TPU v7x, 256 devices: a whole 4x4x8 slice. The times are simulated.
256 devices in a mesh: band: 16 (over y_lo, z), dom: 16 (over x, y_hi, core).
Axes of the slice: x: 4, y: 4 (y_hi: 2, y_lo: 2; y = y_hi * 2 + y_lo), z: 8, core: 2. Of those that a mesh axis runs over, the one named last changes fastest.
Arguments:
- wavefunctions: float32 [1024, 64, 16, 128], P('band', 'dom'), may hold values from -6 to 6
- potential: float32 [64, 16, 128], P('dom'), may hold values from -40 to 40
- projectors: float32 [64, 18, 4, 16, 128], P('dom'), may hold values from -0.0625 to 0.0625
- hamiltonian_correction: float32 [64, 18, 18], P('dom'), may hold values from -0.0390625 to 0.0390625
- delta_s: float32 [64, 18, 18], P('dom'), may hold values from -0.0390625 to 0.0390625
- projector_count: int32 [64], P('dom'), may hold values from 1 to 18
Outputs:
- ham: float32 [1024, 1024], P('band')
- correlation: float32 [1024, 1024], P('band')
All inputs are finite; a program needn't handle non-finite values.
Results may differ from a plain program's by a relative error of at most 0.00007.
Values sent between devices are 32-bit elements; how exact they have to be, the bound alone decides.
No kernel may reach another device: no remote copies, remote signals or barrier semaphores. Data moves between devices by JAX's collectives and lax.ppermute only.
A program may use at most 192 MiB of HBM per device.

v0:
```python
import jax
import jax.numpy as jnp
from jax import lax
from jax.experimental import pallas as pl
from jax.experimental.pallas import tpu as pltpu
from jax.sharding import PartitionSpec as P


F32 = jnp.float32
BF16 = jnp.bfloat16
HI = lax.Precision.HIGHEST
VMEM = pl.BlockSpec(memory_space=pltpu.VMEM)
SMEM = pl.BlockSpec(memory_space=pltpu.SMEM)


def lane_of(shape):
    return lax.broadcasted_iota(jnp.int32, shape, len(shape) - 1)


def turn(x, n):
    n = n % 128
    return pltpu.roll(x, n, 1) if n else x


MOVES = [(0, 0)] + [(y, z) for z in (4, 3, -3, 2, -2, 1, -1) for y in (0, 1)] + [(1, 0)]


def band_at(b, move, sign=1):
    return (b // 8 + move[0]) % 2 * 8 + (b + sign * move[1] + 8) % 8


def spread_kernel(wf, out, last, held, ready, sems):
    lane = lane_of((8, 128))
    block = lane // 8

    def fetch(i):
        rows = pl.ds(pl.multiple_of(i * 512, 512), 512)
        return pltpu.make_async_copy(wf.at[rows], held.at[rows], sems.at[i])

    for i in range(8):
        fetch(i).start()

    def body(bg, _):
        fetch(bg).wait()
        for x in range(4):
            v = [held[pl.ds(bg * 512 + x * 16 + y, 8, stride=64), :] for y in range(16)]
            for s in (1, 2, 4, 8):
                low = (block & s) == 0
                nxt = list(v)
                for y in range(16):
                    if not y & s:
                        a, b = v[y], v[y + s]
                        if s == 8:
                            a_high = b_low = turn(jnp.where(low, b, a), 64)
                        else:
                            b_low, a_high = turn(b, s * 8), turn(a, -s * 8)
                        nxt[y] = jnp.where(low, a, b_low)
                        nxt[y + s] = jnp.where(low, a_high, b)
                v = nxt
            rows = pl.ds(pl.multiple_of(x * 64 + bg * 8, 8), 8)
            for k in range(16):
                ready[k, rows, :] = v[k]
        return 0

    lax.fori_loop(0, 8, body, 0)
    one = pltpu.make_async_copy(ready.at[:, :192], out, sems.at[8])
    two = pltpu.make_async_copy(ready.at[:, 192:], last, sems.at[9])
    one.start()
    two.start()
    one.wait()
    two.wait()


def edge_kernel(r, first, below):
    lane = lane_of((32, 128))

    def body(g, _):
        first[g] = r[g, :64, :]
        acc = r[g, :32, :]
        for i in (1, 2, 4, 5, 6):
            at = i % 4 * 64 + i // 4 * 32
            acc = jnp.where(lane % 8 == i, turn(r[g, at : at + 32, :], i), acc)
        below[g] = acc
        return 0

    lax.fori_loop(0, 16, body, 0)


def split(x):
    hi = x.astype(BF16)
    return hi, (x - hi.astype(F32)).astype(BF16)


def dot(a, b):
    return lax.dot_general(a, b, (((1,), (1,)), ((), ())), preferred_element_type=F32)


def slots(e, er, i, j):
    return lax.dot_general(e[:, i], er[:, j], (((0,), (0,)), ((), ())), preferred_element_type=F32)


def place(g):
    return (g % 2) * 8 + g // 2


FIRST = (0, 8, 10)


def couple_kernel(hc, ds, out):
    lane = lane_of((24, 128))
    out[...] = jnp.zeros_like(out)
    for t, m in enumerate((hc, ds)):
        for a in range(4):
            out[t, a, :16, :18] = m[a, :16, :]
            out[t, a, 16:, :18] = m[a, 10:18, :]
            v = out[t, a]
            out[t, a] = jnp.where(lane < 16, v, jnp.where(lane < 24, turn(v, 6), jnp.zeros_like(v)))


def coef_kernel(ids, count, wf, proj, sym, potential, last, pot, *refs):
    outs, (rows, padded, plain) = refs[:16], refs[16:]
    for x in range(4):
        v = pltpu.roll(potential[x], lax.rem(128 - 8 * ids[0], 128), 1)
        own = lane_of((16, 128)) // 8 == lax.broadcasted_iota(jnp.int32, (16, 128), 0)
        v = jnp.where(own, pltpu.roll(v, 0, 1, stride=8, stride_axis=0), jnp.zeros_like(v))
        pot[x : x + 1, :] = jnp.sum(v, axis=0, keepdims=True)

    def add(i, acc):
        p, w = [], []
        for xy in (4 * i, 4 * i + 1, 4 * i + 2, 4 * i + 3):
            p.append(jnp.concatenate([proj[pl.ds((18 * a + f) * 64 + xy, 8, stride=64), :] for a in range(4) for f in FIRST], axis=0))
            w.append(wf[pl.ds(xy, 64, stride=64), :])
        ph, plo = split(jnp.concatenate(p, axis=1))
        wh, wlo = split(jnp.concatenate(w, axis=1))
        return acc + (dot(ph, wh) + dot(ph, wlo) + dot(plo, wh))

    acc = lax.fori_loop(0, 16, add, jnp.zeros((96, 64), F32))
    row = lax.broadcasted_iota(jnp.int32, (24, 64), 0)
    slot = jnp.where(row < 16, row, row - 6)
    rows[...] = jnp.zeros_like(rows)
    plain[...] = jnp.zeros_like(plain)
    for a in range(4):
        kept = (slot < count[a]) & ((row < 16) | (slot >= 16))
        c = jnp.where(kept, acc[a * 24 : a * 24 + 24], jnp.zeros((24, 64), F32))
        padded[...] = jnp.zeros_like(padded)
        padded[:24, :] = c
        found = [c]
        for t in range(2):
            m = sym[t, a]
            right = jnp.dot(m, padded[...], precision=HI, preferred_element_type=F32)
            left = lax.dot_general(m, c, (((0,), (0,)), ((), ())), precision=HI, preferred_element_type=F32)
            found.append(0.5 * (right + left[:24]))
        for t, v in enumerate(found):
            plain[t, 18 * a : 18 * a + 16, :] = v[:16]
            plain[t, 18 * a + 16 : 18 * a + 18, :] = v[22:]
    for k in range(16):
        own = slice(5 * k, 5 * k + 5)
        rows[k, 0:5, :64] = plain[0, own, :]
        rows[k, 5:8, :64] = plain[1, 5 * k : 5 * k + 3, :]
        rows[k, 0:2, 64:] = plain[1, 5 * k + 3 : 5 * k + 5, :]
        rows[k, 2:7, 64:] = plain[2, own, :]
    lane = lane_of((8, 128))
    for m, out in zip(MOVES, outs):
        to = band_at(ids[0], m)
        out[:8, :] = rows[to]
        out[16:, :] = last[to]
        after = lax.rem(to + 1, 16)
        acc = last[after, :8, :]
        for i in range(1, 8):
            acc = jnp.where(lane % 8 == i, turn(last[after, i * 8 : i * 8 + 8, :], i), acc)
        out[8:16, :] = acc


def corr_kernel(r, pot, ah, al, part, ce, co):
    volume = 1.0 / (512 * 256)
    lane = lane_of((64, 128))
    zero = jnp.zeros((64, 128), F32)

    def prepare(g, _):
        to = pl.ds(pl.multiple_of(place(g) * 64, 64), 64)
        for x in range(3):
            cols = slice(x * 128, (x + 1) * 128)
            p = r[g, x * 64 : (x + 1) * 64, :]
            ah[to, cols], al[to, cols] = split(p)
            beside = turn(p, -8) + jnp.where(lane % 8 == 7, zero, turn(p, -1))
            if x < 2:
                beside = beside + r[g, (x + 1) * 64 : (x + 2) * 64, :]
            part[to, cols] = (1.5 + 0.5 * pot[x : x + 1, :]) * p - 0.5 * beside
        return 0

    lax.fori_loop(0, 16, prepare, 0)

    def corr(i, j):
        i, j = slice(i, i + 256), slice(j, j + 256)
        acc = dot(ah[i, :], ah[j, :]) + dot(ah[i, :], al[j, :]) + dot(al[i, :], ah[j, :])
        return acc * volume

    for q in range(2):
        for n, (i, j) in enumerate(((0, 0), (256, 0), (256, 256))):
            ce[q, n] = corr(q * 512 + i, q * 512 + j)
    for i in (0, 256):
        for j in (0, 256):
            co[i : i + 256, j : j + 256] = corr(512 + i, j)


def gram(which, ah, al, ph, lo, er, eh, es, ce, co, out, c, on):
    volume = 1.0 / (512 * 256)
    low = lane_of((64, 128)) < 64

    def ham(i, j):
        i, j = slice(i, i + 256), slice(j, j + 256)
        acc = dot(ph[i, :], ah[j, :]) + dot(ph[i, :], al[j, :]) + dot(lo[i, :], ah[j, :])
        acc += dot(ah[i, :], ph[j, :]) + dot(al[i, :], ph[j, :]) + dot(ah[i, :], lo[j, :])
        return acc + slots(eh, er, i, j)

    def corr(v, i, j):
        i, j, x = slice(i, i + 256), slice(j, j + 256), slice(384, 512)
        acc = dot(ah[i, x], ah[j, x]) + dot(ah[i, x], al[j, x]) + dot(al[i, x], ah[j, x])
        return v + acc * volume + slots(es, er, i, j)

    def tiles(e, f, t, get):
        for j in range(4):
            if f % 2:
                lower, upper = get(2 * j + 1, (f - 2 * j - 1) % 8 // 2), get(2 * j, (f - 2 * j - 1) % 8 // 2)
            else:
                lower, upper = get(2 * j, (f - 2 * j) % 8 // 2), get(2 * j + 1, (f - 2 * j - 2) % 8 // 2)
            out[e, (t + j) * 64 : (t + j) * 64 + 64, :] = jnp.where(low, lower, upper)

    @pl.when(which == 0)
    def _():
        row = lax.broadcasted_iota(jnp.int32, (256, 256), 0)
        col = lax.broadcasted_iota(jnp.int32, (256, 256), 1)
        for q in range(2):
            at = q * 512
            c[q, :256, 256:] = ham(at, at + 256)
            c[q, 256:, :256] = corr(ce[q, 1], at + 256, at)
            for n in range(2):
                here, own = slice(n * 256, n * 256 + 256), corr(ce[q, 2 * n], at + n * 256, at + n * 256)
                c[q, here, here] = jnp.where(row <= col, ham(at + n * 256, at + n * 256), own)
                diagonal = jnp.sum(jnp.where(row == col, own, jnp.zeros_like(own)), axis=0, keepdims=True)
                on[q, n] = jnp.broadcast_to(diagonal, (8, 256))
        for e in range(8):
            for q in range(2):
                tiles(e, (e - q) % 8, q * 4, lambda m, n: c[q, m * 64 : m * 64 + 64, n * 128 : n * 128 + 128])
            m = e // 2
            cols = slice(m // 2 * 128, m // 2 * 128 + 128)
            a, b = on[e % 2, 0, :, cols], on[e % 2, 1, :, cols]
            if m % 2:
                a = turn(a, 64)
            else:
                b = turn(b, 64)
            out[e, 512:, :] = jnp.where(low[:8], a, b)

    @pl.when(which == 1)
    def _():
        for i in (0, 256):
            for j in (0, 256):
                c[0, i : i + 256, j : j + 256] = ham(i, 512 + j)
                c[1, i : i + 256, j : j + 256] = corr(co[i : i + 256, j : j + 256], 512 + i, j)
        for e in range(8):
            tiles(e, e, 0, lambda m, n: c[0, m * 64 : m * 64 + 64, n * 128 : n * 128 + 128])
            tiles(e, e, 4, lambda m, n: c[1, m * 64 : m * 64 + 64, n * 128 : n * 128 + 128])
            out[e, 512:, :] = jnp.zeros((8, 128), F32)


def send_kernel(ids, part, xh, zh, pot, th, tl, ce, co, *refs):
    came, (out, ph, lo, ah, al, er, eh, es, c, on, last, cc) = refs[:16], refs[16:]
    volume = 1.0 / (512 * 256)
    lane = lane_of((64, 128))
    for m, v in zip(MOVES, came):
        g = band_at(ids[0], m, -1)
        cc[g] = v[:8, :]
        last[g] = v[8:, :]
    half = lane_of((8, 128)) < 64
    none = jnp.zeros((3, 128), F32)
    for n in range(8):
        a, b = cc[4 * n % 16 + n // 4], cc[(4 * n + 2) % 16 + n // 4]
        x, y = jnp.where(half, a, turn(b, 64)), jnp.where(half, turn(a, 64), b)
        for t, (e, v) in enumerate(((er, x[:5]), (eh, jnp.concatenate([x[5:], y[:2]], axis=0)), (es, y[2:7]))):
            hi, mid = [w.astype(F32) for w in split(jnp.concatenate([v, none], axis=0))]
            zero = jnp.zeros_like(hi)
            terms = [hi, hi, mid, zero] if t else [hi, mid, hi, zero]
            e[:, n * 128 : n * 128 + 128] = jnp.concatenate(terms, axis=0).astype(BF16)

    def prepare(g, _):
        to = pl.ds(pl.multiple_of(place(g) * 64, 64), 64)
        two = zh[g]
        ext = jnp.concatenate([two, turn(two, -4)], axis=0)
        end = lane % 8 == 7
        p = last[g, 8:, :]
        ah[to, :384], al[to, :384] = th[to, :], tl[to, :]
        ah[to, 384:], al[to, 384:] = split(p)
        for x in range(3):
            cols = slice(x * 128, (x + 1) * 128)
            beside = jnp.where(end, turn(ext, 7 - x), jnp.zeros((64, 128), F32))
            if x == 2:
                beside = beside + p
            ph[to, cols], lo[to, cols] = split((part[to, cols] - 0.5 * beside) * volume)
        after = last[g, :8, :]
        after = jnp.concatenate([turn(after, 7 - i) for i in range(8)], axis=0)
        beside = xh[g] + turn(p, -8) + jnp.where(end, after, turn(p, -1))
        phi = (1.5 + 0.5 * pot[3:4, :]) * p - 0.5 * beside
        ph[to, 384:], lo[to, 384:] = split(phi * volume)
        return 0

    lax.fori_loop(0, 16, prepare, 0)
    gram(1 - lax.rem(ids[1], 2), ah, al, ph, lo, er, eh, es, ce, co, out, c, on)


def keep_kernel(ids, ph, lo, ah, al, er, eh, es, ce, co, out, c, on):
    gram(lax.rem(ids[1], 2), ah, al, ph, lo, er, eh, es, ce, co, out, c, on)


def first_kernel(ids, keep, mate, s1, s2, s3, own):
    d = ids[1]
    north, x, h = lax.rem(d, 2) == 1, d // 4, lax.rem(d // 2, 2)

    def total(ref, i, across, along):
        e = jnp.where(north, along, across)
        ref[i] = keep[e] + mate[e]

    def part(dx, y):
        return lax.rem(x + dx, 4) * 2 + y

    for i in range(2):
        total(s1, i, part(1, i), part(i, 1 - h))
        total(s2, i, part(3, i), part(2 + i, 1 - h))
        total(own, i, part(0, i), part(i, h))
        total(own, 2 + i, part(0, i), part(2 + i, h))
        total(s3, i, part(2, i), part(2, i))


def second_kernel(ids, own, r1, r2, r3, keep, s1, s2, s3):
    d = ids[1]
    north, h = lax.rem(d, 2) == 1, lax.rem(d // 2, 2)

    @pl.when(jnp.logical_not(north))
    def _():
        def total(i):
            return own[i] + r1[i] + r2[i] + r3[i]

        keep[...] = total(h)
        s1[...] = total(1 - h)

    @pl.when(north)
    def _():
        keep[...] = own[0] + r1[0]
        s1[...] = own[1] + r1[1]
        s3[...] = own[2] + r2[0]
        s2[...] = own[3] + r2[1]


def rows_kernel(ids, keep, r1, r2, r3, out, total):
    d = ids[1]
    low = lane_of((64, 128)) < 64
    total[...] = keep[...] + r1[...]

    @pl.when(lax.rem(d, 2) == 1)
    def _():
        total[...] = total[...] + (r2[...] + r3[...])

    e = d // 2
    even = 1 - lax.rem(d, 2)

    def block(g, upper):
        m, p = g // 2, lax.rem(g, 2)
        t = total[pl.ds(pl.multiple_of((p * 4 + m // 2) * 64, 64), 64), :]
        half = lax.rem(m + e + even * p, 2)
        return jnp.where(half == upper, t, pltpu.roll(t, 64, 1))

    for g in range(16):
        h = lax.rem(d - g + 16, 16)
        own = jnp.broadcast_to(total[512:513, :], (64, 128))
        own = own if g >= 8 else turn(own, 64)
        out[g] = jnp.where(low, block(jnp.int32(g), 0), jnp.where(h == g, own, block(h, 1)))


def finish_kernel(ids, parts, out):
    b, d = ids[0], ids[1]
    h = lax.rem(d - b + 16, 16)
    t = parts[0]
    for s in range(1, 16):
        t = t + parts[s]
    low = lane_of((64, 128)) < 64
    both = jnp.concatenate([t, t], axis=0).T
    left, right, other = both[:64], both[64:], turn(t, 64)
    upper = jnp.where(low, t, right)
    lower = jnp.where(low, right, other)
    row, col = lax.broadcasted_iota(jnp.int32, (64, 128), 0), lane_of((64, 128)) % 64
    own = jnp.where(low, jnp.where(row <= col, t, left), jnp.where(row > col, other, jnp.where(row < col, left, t)))
    first = jnp.where(lax.rem(d, 2) == 1, lax.rem(b, 2), (b > h).astype(jnp.int32)) == 0
    out[...] = jnp.where(b == h, own, jnp.where(first, upper, lower))


def join_kernel(a, b, c, d, out):
    for i, v in enumerate((a, b, c, d)):
        out[i] = v[...]


def assemble_kernel(ids, own, r1, r2, r3, ham, corr, parts):
    b, d = ids[0], ids[1]
    low = lane_of((64, 128)) < 64
    for i, v in enumerate((own, r1, r2, r3)):
        parts[4 * i : 4 * i + 4] = v[...]

    def piece(h):
        at = lax.rem(h + b, 16)
        ahead = lax.rem(at // 4 - d // 4 + 4, 4)
        return parts[ahead * 4 + (lax.rem(at, 4) ^ lax.rem(d, 4))]

    for j in range(8):
        t0, t1 = piece(2 * j), piece(2 * j + 1)
        cols = slice(j * 128, (j + 1) * 128)
        ham[:, cols] = jnp.where(low, t0, turn(t1, 64))
        corr[:, cols] = jnp.where(low, turn(t0, 64), t1)


def call(kernel, args, outs, scratch=(), flops=0, mib=8):
    specs = [SMEM if a.dtype == jnp.int32 else VMEM for a in args]
    size = sum(a.size * a.dtype.itemsize for a in (*args, *outs))
    single = len(outs) == 1
    return pl.pallas_call(
        kernel,
        out_shape=outs[0] if single else outs,
        in_specs=specs,
        out_specs=VMEM if single else [VMEM] * len(outs),
        scratch_shapes=scratch,
        compiler_params=pltpu.CompilerParams(vmem_limit_bytes=mib * 1024 * 1024),
        cost_estimate=pl.CostEstimate(flops=flops or 8 * size, bytes_accessed=size, transcendentals=0),
    )(*args)


def shape(*dims, dtype=F32):
    return jax.ShapeDtypeStruct(dims, dtype)


def moves(south, north):
    pairs = []
    for d in range(16):
        x, h, c = d // 4, d // 2 % 2, d % 2
        step = north if c else south
        if step:
            pairs.append((d, (x + step[0]) % 4 * 4 + (h + step[1]) % 2 * 2 + c))
    return pairs


def reduced_over_dom(ids, keep, mate):
    piece = (520, 128)
    sends = call(first_kernel, (ids, keep, mate), [shape(n, *piece) for n in (2, 2, 2, 4)], mib=16)
    steps = (((1, 0), (0, 1)), ((3, 0), (0, 1)), ((2, 0), None))
    got = [lax.ppermute(v, "dom", moves(*s)) for v, s in zip(sends, steps)]
    keep, *sends = call(second_kernel, (ids, sends[3], *got), [shape(*piece)] * 4, mib=12)
    steps = (((0, 1), (1, 0)), (None, (3, 0)), (None, (2, 0)))
    got = [lax.ppermute(v, "dom", moves(*s)) for v, s in zip(sends, steps)]
    return call(rows_kernel, (ids, keep, *got), (shape(16, 64, 128),), [pltpu.VMEM(piece, F32)], mib=8)


def on_device(wavefunctions, potential, projectors, hamiltonian_correction, delta_s, projector_count):
    bands, cx, ny, nz = wavefunctions.shape
    atoms, slots = hamiltonian_correction.shape[:2]
    b, d = lax.axis_index("band"), lax.axis_index("dom")
    ids = jnp.stack([b, d]).astype(jnp.int32)

    flat = cx * ny
    wf = wavefunctions.reshape(bands * flat, nz)
    parts, last = pl.pallas_call(
        spread_kernel,
        out_shape=[shape(16, 3 * bands, 128), shape(16, bands, 128)],
        in_specs=[pl.BlockSpec(memory_space=pltpu.HBM)],
        out_specs=[pl.BlockSpec(memory_space=pltpu.HBM)] * 2,
        scratch_shapes=[
            pltpu.VMEM((bands * flat, nz), F32),
            pltpu.VMEM((16, cx * bands, 128), F32),
            pltpu.SemaphoreType.DMA((10,)),
        ],
        compiler_params=pltpu.CompilerParams(vmem_limit_bytes=61 * 1024 * 1024),
    )(wf)
    slab = lax.all_to_all(parts, "band", 0, 0, tiled=True)

    proj = projectors.reshape(atoms * slots * flat, nz)
    wf, proj, potential, hamiltonian_correction, delta_s, parts = lax.optimization_barrier(
        (wf, proj, potential, hamiltonian_correction, delta_s, parts)
    )
    sym = call(couple_kernel, (hamiltonian_correction, delta_s), (shape(2, atoms, 24, 128),), mib=2)
    pot, *came = call(
        coef_kernel,
        (ids, projector_count, wf, proj, sym, potential, last),
        [shape(cx, nz)] + [shape(16 + bands, 128)] * 16,
        [pltpu.VMEM((16, 8, 128), F32), pltpu.VMEM((128, bands), F32), pltpu.VMEM((3, 80, bands), F32)],
    )
    for i, move in enumerate(MOVES):
        if i:
            came[i] = lax.ppermute(came[i], "band", [(j, band_at(j, move)) for j in range(16)])
    back = [((i + 1) % 16, i) for i in range(16)]
    first, below = call(edge_kernel, (slab,), [shape(16, bands, 128), shape(16, bands // 2, 128)], mib=4)
    ahead, above = lax.ppermute(first, "dom", back), lax.ppermute(below, "band", back)
    m = 16 * bands
    three, wide = shape(m, 384, dtype=BF16), shape(m, 512, dtype=BF16)
    ext = [shape(32, m, dtype=BF16)] * 3
    work = 2 * m * m * 512
    quads = [pltpu.VMEM((2, 512, 512), F32), pltpu.VMEM((2, 2, 8, 256), F32)]
    ah, al, part, ce, co = call(
        corr_kernel,
        (slab, pot),
        [three, three, shape(m, 384), shape(2, 3, 256, 256), shape(512, 512)],
        flops=3 * work,
        mib=16,
    )
    ahead, above, ah, *came = lax.optimization_barrier((ahead, above, ah, *came))
    parts = shape(8, 520, 128)
    send, *rest = call(
        send_kernel,
        (ids, part, ahead, above, pot, ah, al, ce, co, *came),
        [parts, wide, wide, wide, wide, *ext],
        quads + [pltpu.VMEM((16, 72, 128), F32), pltpu.VMEM((16, 8, 128), F32)],
        3 * work,
        22,
    )
    mate = lax.ppermute(send, "dom", [(i, i ^ 1) for i in range(16)])
    keep = call(keep_kernel, (ids, *rest, ce, co), [parts], quads, 3 * work, 18)
    parts = reduced_over_dom(ids, keep, mate)
    parts = lax.all_to_all(parts, "band", 0, 0, tiled=True)
    own = call(finish_kernel, (ids, parts), (shape(64, 128),))
    near = [lax.ppermute(own, "dom", [(i, i ^ j) for i in range(16)]) for j in (1, 2, 3)]
    own = call(join_kernel, (own, *near), (shape(4, 64, 128),))
    far = [lax.ppermute(own, "dom", [((i + 4 * j) % 16, i) for i in range(16)]) for j in (1, 2, 3)]
    return call(
        assemble_kernel,
        (ids, own, *far),
        (shape(64, 1024), shape(64, 1024)),
        [pltpu.VMEM((16, 64, 128), F32)],
    )


def solution(mesh):
    placed = (
        P("band", "dom", None, None),
        P("dom", None, None),
        P("dom", None, None, None, None),
        P("dom", None, None),
        P("dom", None, None),
        P("dom"),
    )
    return jax.shard_map(
        on_device,
        mesh=mesh,
        in_specs=placed,
        out_specs=(P("band", None), P("band", None)),
        check_vma=False,
    )
```

profile of v0, /device:TPU:1, one launch (start us, length us, event | category | flops | bytes accessed | tf_op | source)
XLA Modules:
  0.0 187.7 jit_solution(14053260236544789950)
XLA Ops:
  0.6 6.1 %shard_map.77 = (f32[16,192,128]{2,1,0:T(8,128)}, f32[16,64,128]{2,1,0:T(8,128)}) custom-call(f32[4096,128]{1,0:T(8,128)} %bitcast.4), custom_call_target="tpu_custom_call" | custom-call | tf_op jit(solution)/shard_map/pallas_call | solution.py:466
  6.8 10.4 %all-to-all-start = ((f32[16,192,128]{2,1,0:T(8,128)}), f32[16,192,128]{2,1,0:T(8,128)}, u32[]{:S(2)}, u32[]{:S(2)}) async-start(f32[16,192,128]{2,1,0:T(8,128)} %get-tuple-element.68), calls=%async_computation | async-start | bytes 3145728 | tf_op jit(solution)/shard_map/all_to_all | solution.py:478
  17.5 36.3 %all-to-all-done.r = f32[16,192,128]{2,1,0:T(8,128)} async-done(((f32[16,192,128]{2,1,0:T(8,128)}), f32[16,192,128]{2,1,0:T(8,128)}, u32[]{:S(2)}, u32[]{:S(2)}) %all-to-all-start) | async-done | bytes 1572896 | tf_op jit(solution)/shard_map/all_to_all | solution.py:478
  53.7 2.9 %shard_map.81 = (f32[16,64,128]{2,1,0:T(8,128)S(1)}, f32[16,32,128]{2,1,0:T(8,128)S(1)}) custom-call(f32[16,192,128]{2,1,0:T(8,128)} %all-to-all-done.r), custom_call_target="tpu_custom_call" | custom-call | flops 18874368 | bytes 2359296 | tf_op jit(solution)/shard_map/pallas_call | solution.py:422
  56.6 2.7 %collective-permute-start = (f32[16,64,128]{2,1,0:T(8,128)S(1)}, f32[16,64,128]{2,1,0:T(8,128)S(1)}, u32[]{:S(2)}, u32[]{:S(2)}) collective-permute-start(f32[16,64,128]{2,1,0:T(8,128)S(1)} %get-tuple-element.77), channel_id=1, source_target_pairs={{1,0},{2,1},{3,2},{4,3},{5,4},{6,5},{7,6},{8,7},{9,8},{10,9},{11,1... | collective-permute-start | bytes 1572872 | tf_op jit(solution)/shard_map/ppermute | solution.py:496
  59.4 1.7 copy-done.1
  61.1 7.6 %shard_map.79 = (f32[4,128]{1,0:T(4,128)S(1)}, f32[80,128]{1,0:T(8,128)S(1)}, f32[80,128]{1,0:T(8,128)S(1)}, f32[80,128]{1,0:T(8,128)S(1)}, f32[80,128]{1,0:T(8,...) custom-call(s32[2]{0:T(128)S(1)} %pad_add_fusion.ids, ...), custom_call_target="tpu_custom_call" | custom-call | flops 46153920 | bytes 5769240 | tf_op jit(solution)/shard_map/pallas_call | solution.py:422
  68.7 2.3 %collective-permute-start.2 = (f32[80,128]{1,0:T(8,128)S(1)}, f32[80,128]{1,0:T(8,128)S(1)}, u32[]{:S(2)}, u32[]{:S(2)}) collective-permute-start(f32[80,128]{1,0:T(8,128)S(1)} %get-tuple-element.81), channel_id=1, source_target_pairs={{0,64},{16,80},{32,96},{48,112},{64,0},{80,16},{96,32},{112,48},{1... | collective-permute-start | bytes 122888 | tf_op jit(solution)/shard_map/ppermute | solution.py:493
  71.1 2.9 %collective-permute-start.3 = (f32[80,128]{1,0:T(8,128)S(1)}, f32[80,128]{1,0:T(8,128)S(1)}, u32[]{:S(2)}, u32[]{:S(2)}) collective-permute-start(f32[80,128]{1,0:T(8,128)S(1)} %get-tuple-element.82), channel_id=1, source_target_pairs={{0,192},{16,208},{32,224},{48,240},{64,128},{80,144},{96,160},{112... | collective-permute-start | bytes 122888 | tf_op jit(solution)/shard_map/ppermute | solution.py:493
  73.9 3.2 %collective-permute-start.4 = (f32[80,128]{1,0:T(8,128)S(1)}, f32[80,128]{1,0:T(8,128)S(1)}, u32[]{:S(2)}, u32[]{:S(2)}) collective-permute-start(f32[80,128]{1,0:T(8,128)S(1)} %get-tuple-element.83), channel_id=1, source_target_pairs={{0,48},{16,64},{32,80},{48,96},{64,112},{80,0},{96,16},{112,32},{1... | collective-permute-start | bytes 122888 | tf_op jit(solution)/shard_map/ppermute | solution.py:493
  77.1 2.1 %collective-permute-start.5 = (f32[80,128]{1,0:T(8,128)S(1)}, f32[80,128]{1,0:T(8,128)S(1)}, u32[]{:S(2)}, u32[]{:S(2)}) collective-permute-start(f32[80,128]{1,0:T(8,128)S(1)} %get-tuple-element.84), channel_id=1, source_target_pairs={{0,176},{16,192},{32,208},{48,224},{64,240},{80,128},{96,144},{112... | collective-permute-start | bytes 122888 | tf_op jit(solution)/shard_map/ppermute | solution.py:493
  79.2 2.4 %collective-permute-start.6 = (f32[80,128]{1,0:T(8,128)S(1)}, f32[80,128]{1,0:T(8,128)S(1)}, u32[]{:S(2)}, u32[]{:S(2)}) collective-permute-start(f32[80,128]{1,0:T(8,128)S(1)} %get-tuple-element.85), channel_id=1, source_target_pairs={{0,80},{16,96},{32,112},{48,0},{64,16},{80,32},{96,48},{112,64},{1... | collective-permute-start | bytes 122888 | tf_op jit(solution)/shard_map/ppermute | solution.py:493
  81.6 2.2 %collective-permute-start.7 = (f32[80,128]{1,0:T(8,128)S(1)}, f32[80,128]{1,0:T(8,128)S(1)}, u32[]{:S(2)}, u32[]{:S(2)}) collective-permute-start(f32[80,128]{1,0:T(8,128)S(1)} %get-tuple-element.86), channel_id=1, source_target_pairs={{0,208},{16,224},{32,240},{48,128},{64,144},{80,160},{96,176},{112... | collective-permute-start | bytes 122888 | tf_op jit(solution)/shard_map/ppermute | solution.py:493
  84.0 1.5 collective-permute-done.5.refs_4_
  85.5 1.9 %collective-permute-start.9 = (f32[80,128]{1,0:T(8,128)S(1)}, f32[80,128]{1,0:T(8,128)S(1)}, u32[]{:S(2)}, u32[]{:S(2)}) collective-permute-start(f32[80,128]{1,0:T(8,128)S(1)} %get-tuple-element.88), channel_id=1, source_target_pairs={{0,160},{16,176},{32,192},{48,208},{64,224},{80,240},{96,128},{112... | collective-permute-start | bytes 122888 | tf_op jit(solution)/shard_map/ppermute | solution.py:493
  87.5 2.0 %collective-permute-start.10 = (f32[80,128]{1,0:T(8,128)S(1)}, f32[80,128]{1,0:T(8,128)S(1)}, u32[]{:S(2)}, u32[]{:S(2)}) collective-permute-start(f32[80,128]{1,0:T(8,128)S(1)} %get-tuple-element.89), channel_id=1, source_target_pairs={{0,96},{16,112},{32,0},{48,16},{64,32},{80,48},{96,64},{112,80},{1... | collective-permute-start | bytes 122888 | tf_op jit(solution)/shard_map/ppermute | solution.py:493
  89.5 2.3 %collective-permute-start.11 = (f32[80,128]{1,0:T(8,128)S(1)}, f32[80,128]{1,0:T(8,128)S(1)}, u32[]{:S(2)}, u32[]{:S(2)}) collective-permute-start(f32[80,128]{1,0:T(8,128)S(1)} %get-tuple-element.90), channel_id=1, source_target_pairs={{0,224},{16,240},{32,128},{48,144},{64,160},{80,176},{96,192},{112... | collective-permute-start | bytes 122888 | tf_op jit(solution)/shard_map/ppermute | solution.py:493
  91.8 0.8 collective-permute-start.12
  93.1 2.6 %collective-permute-start.14 = (f32[80,128]{1,0:T(8,128)S(1)}, f32[80,128]{1,0:T(8,128)S(1)}, u32[]{:S(2)}, u32[]{:S(2)}) collective-permute-start(f32[80,128]{1,0:T(8,128)S(1)} %get-tuple-element.93), channel_id=1, source_target_pairs={{0,112},{16,0},{32,16},{48,32},{64,48},{80,64},{96,80},{112,96},{1... | collective-permute-start | bytes 122888 | tf_op jit(solution)/shard_map/ppermute | solution.py:493
  95.7 1.8 collective-permute-start.15
  97.4 0.9 collective-permute-start.16
  98.4 0.8 collective-permute-start.1
  99.1 5.5 %shard_map.80 = (bf16[1024,384]{1,0:T(8,128)(2,1)S(1)}, bf16[1024,384]{1,0:T(8,128)(2,1)S(1)}, f32[1024,384]{1,0:T(8,128)S(1)}, f32[2,3,256,256]{3,2,1,0:T(8,128)S(1)}, f32[512,512]{1,0:T(8,128)S(1)}) custom-call(f32[16,192,128]{2,1,0:T(8,128)} %all-to-all-done.r, f32[4,128]{1,0:T(4,128)S(1)} %get-tuple-element.75.pot), custom_call_target="tpu_custom_call" | custom-call | flops 3221225472 | bytes 7342080 | tf_op jit(solution)/shard_map/pallas_call | solution.py:422
  104.8 7.0 %shard_map.82 = (f32[8,520,128]{2,1,0:T(8,128)S(1)}, bf16[1024,512]{1,0:T(8,128)(2,1)S(1)}, bf16[1024,512]{1,0:T(8,128)(2,1)S(1)}, bf16[1024,512]{1,0:T(8,128)(2...) custom-call(s32[2]{0:T(128)S(1)} %pad_add_fusion.ids, ...), custom_call_target="tpu_custom_call" | custom-call | flops 3221225472 | bytes 13731848 | tf_op jit(solution)/shard_map/pallas_call | solution.py:422
  111.8 7.0 %collective-permute-start.17 = (f32[8,520,128]{2,1,0:T(8,128)S(1)}, f32[8,520,128]{2,1,0:T(8,128)S(1)}, u32[]{:S(2)}, u32[]{:S(2)}) collective-permute-start(f32[8,520,128]{2,1,0:T(8,128)S(1)} %get-tuple-element.125), channel_id=1, source_target_pairs={{0,1},{1,0},{2,3},{3,2},{4,5},{5,4},{6,7},{7,6},{8,9},{9,8},{10,11... | collective-permute-start | bytes 6389768 | tf_op jit(solution)/shard_map/ppermute | solution.py:519
  118.8 3.3 %shard_map.83.keep = f32[8,520,128]{2,1,0:T(8,128)S(1)} custom-call(s32[2]{0:T(128)S(1)} %pad_add_fusion.ids, bf16[1024,512]{1,0:T(8,128)(2,1)S(1)} %get-tuple-element.118.ph, bf16[1024,512]{1,0:T(8,128)(2,1)S(1)} %get-tuple-element.119.lo, bf16[1024,512]{1,0:T(8,128)(2,1)S(1)} %get-tuple-element.120.ah, bf16[1024,512]{1,0:T(8,128)(2,1)S(1)} %get-tuple-element.121.al, ...), custom_call_target="tpu_custom_call" | custom-call | flops 3221225472 | bytes 9142280 | tf_op jit(solution)/shard_map/pallas_call | solution.py:422
  122.6 0.8 shard_map.84
  123.5 3.0 %collective-permute-start.19 = (f32[2,520,128]{2,1,0:T(8,128)S(1)}, f32[2,520,128]{2,1,0:T(8,128)S(1)}, u32[]{:S(2)}, u32[]{:S(2)}) collective-permute-start(f32[2,520,128]{2,1,0:T(8,128)S(1)} %get-tuple-element.128), channel_id=1, source_target_pairs={{0,12},{1,3},{2,14},{3,1},{4,0},{5,7},{6,2},{7,5},{8,4},{9,11},{10... | collective-permute-start | bytes 1597448 | tf_op jit(solution)/shard_map/ppermute | solution.py:451
  126.5 0.7 collective-permute-start.20
  127.2 6.0 %collective-permute-done.18.r1 = f32[2,520,128]{2,1,0:T(8,128)S(1)} collective-permute-done((f32[2,520,128]{2,1,0:T(8,128)S(1)}, f32[2,520,128]{2,1,0:T(8,128)S(1)}, u32[]{:S(2)}, u32[]{:S(2)}) %collective-permute-start.18) | collective-permute-done | bytes 532512 | tf_op jit(solution)/shard_map/ppermute | solution.py:451
  133.2 6.0 %collective-permute-done.19.r2 = f32[2,520,128]{2,1,0:T(8,128)S(1)} collective-permute-done((f32[2,520,128]{2,1,0:T(8,128)S(1)}, f32[2,520,128]{2,1,0:T(8,128)S(1)}, u32[]{:S(2)}, u32[]{:S(2)}) %collective-permute-start.19) | collective-permute-done | bytes 532512 | tf_op jit(solution)/shard_map/ppermute | solution.py:451
  139.2 0.7 shard_map.85
  139.9 4.6 %collective-permute-start.22 = (f32[520,128]{1,0:T(8,128)S(1)}, f32[520,128]{1,0:T(8,128)S(1)}, u32[]{:S(2)}, u32[]{:S(2)}) collective-permute-start(f32[520,128]{1,0:T(8,128)S(1)} %get-tuple-element.132), channel_id=1, source_target_pairs={{1,13},{3,15},{5,1},{7,3},{9,5},{11,7},{13,9},{15,11},{17,29},{19,... | collective-permute-start | bytes 798728 | tf_op jit(solution)/shard_map/ppermute | solution.py:454
  144.5 1.9 %collective-permute-start.23 = (f32[520,128]{1,0:T(8,128)S(1)}, f32[520,128]{1,0:T(8,128)S(1)}, u32[]{:S(2)}, u32[]{:S(2)}) collective-permute-start(f32[520,128]{1,0:T(8,128)S(1)} %get-tuple-element.133), channel_id=1, source_target_pairs={{1,9},{3,11},{5,13},{7,15},{9,1},{11,3},{13,5},{15,7},{17,25},{19,... | collective-permute-start | bytes 798728 | tf_op jit(solution)/shard_map/ppermute | solution.py:454
  146.7 4.0 %collective-permute-done.22.r2 = f32[520,128]{1,0:T(8,128)S(1)} collective-permute-done((f32[520,128]{1,0:T(8,128)S(1)}, f32[520,128]{1,0:T(8,128)S(1)}, u32[]{:S(2)}, u32[]{:S(2)}) %collective-permute-start.22) | collective-permute-done | bytes 266272 | tf_op jit(solution)/shard_map/ppermute | solution.py:454
  150.7 2.5 %collective-permute-done.23.r3 = f32[520,128]{1,0:T(8,128)S(1)} collective-permute-done((f32[520,128]{1,0:T(8,128)S(1)}, f32[520,128]{1,0:T(8,128)S(1)}, u32[]{:S(2)}, u32[]{:S(2)}) %collective-permute-start.23) | collective-permute-done | bytes 266272 | tf_op jit(solution)/shard_map/ppermute | solution.py:454
  153.2 1.0 shard_map.86
  154.2 16.4 %all_to_all.10.parts = f32[16,64,128]{2,1,0:T(8,128)S(1)} all-to-all(f32[16,64,128]{2,1,0:T(8,128)S(1)} %shard_map.86), channel_id=1, replica_groups=mesh['band'=16,'dom'=16] {'band'}, dimensions={0} | all-to-all | bytes 1048576 | tf_op jit(solution)/shard_map/all_to_all | solution.py:522
  170.6 0.7 shard_map.87.a
  171.4 0.7 collective-permute-start.25
  172.0 3.0 %collective-permute-start.24 = (f32[64,128]{1,0:T(8,128)S(1)}, f32[64,128]{1,0:T(8,128)S(1)}, u32[]{:S(2)}, u32[]{:S(2)}) collective-permute-start(f32[64,128]{1,0:T(8,128)S(1)} %shard_map.87.a), channel_id=1, source_target_pairs={{0,1},{1,0},{2,3},{3,2},{4,5},{5,4},{6,7},{7,6},{8,9},{9,8},{10,11... | collective-permute-start | bytes 98312 | tf_op jit(solution)/shard_map/ppermute | solution.py:524
  175.0 1.2 collective-permute-done.26.d
  176.2 0.9 collective-permute-start.29
  177.2 3.4 %collective-permute-start.28 = (f32[4,64,128]{2,1,0:T(8,128)S(1)}, f32[4,64,128]{2,1,0:T(8,128)S(1)}, u32[]{:S(2)}, u32[]{:S(2)}) collective-permute-start(f32[4,64,128]{2,1,0:T(8,128)S(1)} %shard_map.88.own), channel_id=1, source_target_pairs={{8,0},{9,1},{10,2},{11,3},{12,4},{13,5},{14,6},{15,7},{0,8},{1,9},... | collective-permute-start | bytes 393224 | tf_op jit(solution)/shard_map/ppermute | solution.py:526
  180.6 1.2 collective-permute-done.29.r3
  181.7 3.5 %collective-permute-done.28.r2 = f32[4,64,128]{2,1,0:T(8,128)S(1)} collective-permute-done((f32[4,64,128]{2,1,0:T(8,128)S(1)}, f32[4,64,128]{2,1,0:T(8,128)S(1)}, u32[]{:S(2)}, u32[]{:S(2)}) %collective-permute-start.28) | collective-permute-done | bytes 131104 | tf_op jit(solution)/shard_map/ppermute | solution.py:526
  185.2 0.9 collective-permute-done.27.r1
  186.1 1.6 shard_map.89
  (45 shorter events, 2.0 us)
Async XLA Ops:
  6.8 10.5 %copy-start.5 = (f32[4,18,18]{2,0,1:T(4,128)S(1)}, f32[4,18,18]{2,0,1:T(4,128)}, u32[]{:S(2)}) copy-start(f32[4,18,18]{2,0,1:T(4,128)} %param.9) | copy-start | bytes 15556
  6.8 10.5 %copy-start.6 = (f32[4,18,18]{2,0,1:T(4,128)S(1)}, f32[4,18,18]{2,0,1:T(4,128)}, u32[]{:S(2)}) copy-start(f32[4,18,18]{2,0,1:T(4,128)} %param.10) | copy-start | bytes 15556
  6.8 52.6 %copy-start = (f32[64,4,16,128]{3,2,1,0:T(8,128)S(1)}, f32[64,4,16,128]{3,2,1,0:T(8,128)}, u32[]{:S(2)}) copy-start(f32[64,4,16,128]{3,2,1,0:T(8,128)} %param.6) | copy-start | bytes 6291460
  6.8 52.6 %copy-start.2 = (f32[16,64,128]{2,1,0:T(8,128)S(1)}, f32[16,64,128]{2,1,0:T(8,128)}, u32[]{:S(2)}) copy-start(f32[16,64,128]{2,1,0:T(8,128)} %get-tuple-element.74.last) | copy-start | bytes 1572868
  6.8 52.6 %copy-start.3 = (f32[4,16,128]{2,1,0:T(8,128)S(1)}, f32[4,16,128]{2,1,0:T(8,128)}, u32[]{:S(2)}) copy-start(f32[4,16,128]{2,1,0:T(8,128)} %potential) | copy-start | bytes 98308
  6.8 52.6 %copy-start.4 = (s32[4]{0:T(128)S(1)}, s32[4]{0:T(128)}, u32[]{:S(2)}) copy-start(s32[4]{0:T(128)} %count.1) | copy-start | bytes 52
  6.8 46.9 %all-to-all-start = ((f32[16,192,128]{2,1,0:T(8,128)}), f32[16,192,128]{2,1,0:T(8,128)}, u32[]{:S(2)}, u32[]{:S(2)}) async-start(f32[16,192,128]{2,1,0:T(8,128)} %get-tuple-element.68), calls=%async_computation | async-start | bytes 3145728 | tf_op jit(solution)/shard_map/all_to_all | solution.py:478
  56.6 48.2 %collective-permute-start = (f32[16,64,128]{2,1,0:T(8,128)S(1)}, f32[16,64,128]{2,1,0:T(8,128)S(1)}, u32[]{:S(2)}, u32[]{:S(2)}) collective-permute-start(f32[16,64,128]{2,1,0:T(8,128)S(1)} %get-tuple-element.77), channel_id=1, source_target_pairs={{1,0},{2,1},{3,2},{4,3},{5,4},{6,5},{7,6},{8,7},{9,8},{10,9},{11,1... | collective-permute-start | bytes 1572872 | tf_op jit(solution)/shard_map/ppermute | solution.py:496
  59.4 1.7 copy-start.1
  68.7 10.5 %collective-permute-start.2 = (f32[80,128]{1,0:T(8,128)S(1)}, f32[80,128]{1,0:T(8,128)S(1)}, u32[]{:S(2)}, u32[]{:S(2)}) collective-permute-start(f32[80,128]{1,0:T(8,128)S(1)} %get-tuple-element.81), channel_id=1, source_target_pairs={{0,64},{16,80},{32,96},{48,112},{64,0},{80,16},{96,32},{112,48},{1... | collective-permute-start | bytes 122888 | tf_op jit(solution)/shard_map/ppermute | solution.py:493
  71.1 10.6 %collective-permute-start.3 = (f32[80,128]{1,0:T(8,128)S(1)}, f32[80,128]{1,0:T(8,128)S(1)}, u32[]{:S(2)}, u32[]{:S(2)}) collective-permute-start(f32[80,128]{1,0:T(8,128)S(1)} %get-tuple-element.82), channel_id=1, source_target_pairs={{0,192},{16,208},{32,224},{48,240},{64,128},{80,144},{96,160},{112... | collective-permute-start | bytes 122888 | tf_op jit(solution)/shard_map/ppermute | solution.py:493
  73.9 9.9 %collective-permute-start.4 = (f32[80,128]{1,0:T(8,128)S(1)}, f32[80,128]{1,0:T(8,128)S(1)}, u32[]{:S(2)}, u32[]{:S(2)}) collective-permute-start(f32[80,128]{1,0:T(8,128)S(1)} %get-tuple-element.83), channel_id=1, source_target_pairs={{0,48},{16,64},{32,80},{48,96},{64,112},{80,0},{96,16},{112,32},{1... | collective-permute-start | bytes 122888 | tf_op jit(solution)/shard_map/ppermute | solution.py:493
  77.1 8.4 %collective-permute-start.5 = (f32[80,128]{1,0:T(8,128)S(1)}, f32[80,128]{1,0:T(8,128)S(1)}, u32[]{:S(2)}, u32[]{:S(2)}) collective-permute-start(f32[80,128]{1,0:T(8,128)S(1)} %get-tuple-element.84), channel_id=1, source_target_pairs={{0,176},{16,192},{32,208},{48,224},{64,240},{80,128},{96,144},{112... | collective-permute-start | bytes 122888 | tf_op jit(solution)/shard_map/ppermute | solution.py:493
  79.2 8.2 %collective-permute-start.6 = (f32[80,128]{1,0:T(8,128)S(1)}, f32[80,128]{1,0:T(8,128)S(1)}, u32[]{:S(2)}, u32[]{:S(2)}) collective-permute-start(f32[80,128]{1,0:T(8,128)S(1)} %get-tuple-element.85), channel_id=1, source_target_pairs={{0,80},{16,96},{32,112},{48,0},{64,16},{80,32},{96,48},{112,64},{1... | collective-permute-start | bytes 122888 | tf_op jit(solution)/shard_map/ppermute | solution.py:493
  81.6 7.9 %collective-permute-start.7 = (f32[80,128]{1,0:T(8,128)S(1)}, f32[80,128]{1,0:T(8,128)S(1)}, u32[]{:S(2)}, u32[]{:S(2)}) collective-permute-start(f32[80,128]{1,0:T(8,128)S(1)} %get-tuple-element.86), channel_id=1, source_target_pairs={{0,208},{16,224},{32,240},{48,128},{64,144},{80,160},{96,176},{112... | collective-permute-start | bytes 122888 | tf_op jit(solution)/shard_map/ppermute | solution.py:493
  83.8 8.0 %collective-permute-start.8 = (f32[80,128]{1,0:T(8,128)S(1)}, f32[80,128]{1,0:T(8,128)S(1)}, u32[]{:S(2)}, u32[]{:S(2)}) collective-permute-start(f32[80,128]{1,0:T(8,128)S(1)} %get-tuple-element.87), channel_id=1, source_target_pairs={{0,32},{16,48},{32,64},{48,80},{64,96},{80,112},{96,0},{112,16},{1... | collective-permute-start | bytes 122888 | tf_op jit(solution)/shard_map/ppermute | solution.py:493
  85.5 7.1 %collective-permute-start.9 = (f32[80,128]{1,0:T(8,128)S(1)}, f32[80,128]{1,0:T(8,128)S(1)}, u32[]{:S(2)}, u32[]{:S(2)}) collective-permute-start(f32[80,128]{1,0:T(8,128)S(1)} %get-tuple-element.88), channel_id=1, source_target_pairs={{0,160},{16,176},{32,192},{48,208},{64,224},{80,240},{96,128},{112... | collective-permute-start | bytes 122888 | tf_op jit(solution)/shard_map/ppermute | solution.py:493
  87.5 5.6 %collective-permute-start.10 = (f32[80,128]{1,0:T(8,128)S(1)}, f32[80,128]{1,0:T(8,128)S(1)}, u32[]{:S(2)}, u32[]{:S(2)}) collective-permute-start(f32[80,128]{1,0:T(8,128)S(1)} %get-tuple-element.89), channel_id=1, source_target_pairs={{0,96},{16,112},{32,0},{48,16},{64,32},{80,48},{96,64},{112,80},{1... | collective-permute-start | bytes 122888 | tf_op jit(solution)/shard_map/ppermute | solution.py:493
  89.5 6.1 %collective-permute-start.11 = (f32[80,128]{1,0:T(8,128)S(1)}, f32[80,128]{1,0:T(8,128)S(1)}, u32[]{:S(2)}, u32[]{:S(2)}) collective-permute-start(f32[80,128]{1,0:T(8,128)S(1)} %get-tuple-element.90), channel_id=1, source_target_pairs={{0,224},{16,240},{32,128},{48,144},{64,160},{80,176},{96,192},{112... | collective-permute-start | bytes 122888 | tf_op jit(solution)/shard_map/ppermute | solution.py:493
  91.8 5.6 %collective-permute-start.12 = (f32[80,128]{1,0:T(8,128)S(1)}, f32[80,128]{1,0:T(8,128)S(1)}, u32[]{:S(2)}, u32[]{:S(2)}) collective-permute-start(f32[80,128]{1,0:T(8,128)S(1)} %get-tuple-element.91), channel_id=1, source_target_pairs={{0,16},{16,32},{32,48},{48,64},{64,80},{80,96},{96,112},{112,0},{1... | collective-permute-start | bytes 122888 | tf_op jit(solution)/shard_map/ppermute | solution.py:493
  92.6 5.7 %collective-permute-start.13 = (f32[80,128]{1,0:T(8,128)S(1)}, f32[80,128]{1,0:T(8,128)S(1)}, u32[]{:S(2)}, u32[]{:S(2)}) collective-permute-start(f32[80,128]{1,0:T(8,128)S(1)} %get-tuple-element.92), channel_id=1, source_target_pairs={{0,144},{16,160},{32,176},{48,192},{64,208},{80,224},{96,240},{112... | collective-permute-start | bytes 122888 | tf_op jit(solution)/shard_map/ppermute | solution.py:493
  93.1 11.6 %collective-permute-start.14 = (f32[80,128]{1,0:T(8,128)S(1)}, f32[80,128]{1,0:T(8,128)S(1)}, u32[]{:S(2)}, u32[]{:S(2)}) collective-permute-start(f32[80,128]{1,0:T(8,128)S(1)} %get-tuple-element.93), channel_id=1, source_target_pairs={{0,112},{16,0},{32,16},{48,32},{64,48},{80,64},{96,80},{112,96},{1... | collective-permute-start | bytes 122888 | tf_op jit(solution)/shard_map/ppermute | solution.py:493
  95.7 9.1 %collective-permute-start.15 = (f32[80,128]{1,0:T(8,128)S(1)}, f32[80,128]{1,0:T(8,128)S(1)}, u32[]{:S(2)}, u32[]{:S(2)}) collective-permute-start(f32[80,128]{1,0:T(8,128)S(1)} %get-tuple-element.94), channel_id=1, source_target_pairs={{0,240},{16,128},{32,144},{48,160},{64,176},{80,192},{96,208},{112... | collective-permute-start | bytes 122888 | tf_op jit(solution)/shard_map/ppermute | solution.py:493
  97.4 7.3 %collective-permute-start.16 = (f32[80,128]{1,0:T(8,128)S(1)}, f32[80,128]{1,0:T(8,128)S(1)}, u32[]{:S(2)}, u32[]{:S(2)}) collective-permute-start(f32[80,128]{1,0:T(8,128)S(1)} %get-tuple-element.95), channel_id=1, source_target_pairs={{0,128},{16,144},{32,160},{48,176},{64,192},{80,208},{96,224},{112... | collective-permute-start | bytes 122888 | tf_op jit(solution)/shard_map/ppermute | solution.py:493
  98.4 6.4 %collective-permute-start.1 = (f32[16,32,128]{2,1,0:T(8,128)S(1)}, f32[16,32,128]{2,1,0:T(8,128)S(1)}, u32[]{:S(2)}, u32[]{:S(2)}) collective-permute-start(f32[16,32,128]{2,1,0:T(8,128)S(1)} %get-tuple-element.78), channel_id=1, source_target_pairs={{16,0},{32,16},{48,32},{64,48},{80,64},{96,80},{112,96},{128,112},... | collective-permute-start | bytes 786440 | tf_op jit(solution)/shard_map/ppermute | solution.py:496
  111.8 10.8 %collective-permute-start.17 = (f32[8,520,128]{2,1,0:T(8,128)S(1)}, f32[8,520,128]{2,1,0:T(8,128)S(1)}, u32[]{:S(2)}, u32[]{:S(2)}) collective-permute-start(f32[8,520,128]{2,1,0:T(8,128)S(1)} %get-tuple-element.125), channel_id=1, source_target_pairs={{0,1},{1,0},{2,3},{3,2},{4,5},{5,4},{6,7},{7,6},{8,9},{9,8},{10,11... | collective-permute-start | bytes 6389768 | tf_op jit(solution)/shard_map/ppermute | solution.py:519
  123.5 9.7 %collective-permute-start.18 = (f32[2,520,128]{2,1,0:T(8,128)S(1)}, f32[2,520,128]{2,1,0:T(8,128)S(1)}, u32[]{:S(2)}, u32[]{:S(2)}) collective-permute-start(f32[2,520,128]{2,1,0:T(8,128)S(1)} %get-tuple-element.127), channel_id=1, source_target_pairs={{0,4},{1,3},{2,6},{3,1},{4,8},{5,7},{6,10},{7,5},{8,12},{9,11},{10... | collective-permute-start | bytes 1597448 | tf_op jit(solution)/shard_map/ppermute | solution.py:451
  123.5 15.6 %collective-permute-start.19 = (f32[2,520,128]{2,1,0:T(8,128)S(1)}, f32[2,520,128]{2,1,0:T(8,128)S(1)}, u32[]{:S(2)}, u32[]{:S(2)}) collective-permute-start(f32[2,520,128]{2,1,0:T(8,128)S(1)} %get-tuple-element.128), channel_id=1, source_target_pairs={{0,12},{1,3},{2,14},{3,1},{4,0},{5,7},{6,2},{7,5},{8,4},{9,11},{10... | collective-permute-start | bytes 1597448 | tf_op jit(solution)/shard_map/ppermute | solution.py:451
  126.5 12.7 %collective-permute-start.20 = (f32[2,520,128]{2,1,0:T(8,128)S(1)}, f32[2,520,128]{2,1,0:T(8,128)S(1)}, u32[]{:S(2)}, u32[]{:S(2)}) collective-permute-start(f32[2,520,128]{2,1,0:T(8,128)S(1)} %get-tuple-element.129), channel_id=1, source_target_pairs={{0,8},{2,10},{4,12},{6,14},{8,0},{10,2},{12,4},{14,6},{16,24},{18,... | collective-permute-start | bytes 1597448 | tf_op jit(solution)/shard_map/ppermute | solution.py:451
  139.8 6.8 %collective-permute-start.21 = (f32[520,128]{1,0:T(8,128)S(1)}, f32[520,128]{1,0:T(8,128)S(1)}, u32[]{:S(2)}, u32[]{:S(2)}) collective-permute-start(f32[520,128]{1,0:T(8,128)S(1)} %get-tuple-element.131), channel_id=1, source_target_pairs={{0,2},{1,5},{2,0},{3,7},{4,6},{5,9},{6,4},{7,11},{8,10},{9,13},{10... | collective-permute-start | bytes 798728 | tf_op jit(solution)/shard_map/ppermute | solution.py:454
  139.9 10.8 %collective-permute-start.22 = (f32[520,128]{1,0:T(8,128)S(1)}, f32[520,128]{1,0:T(8,128)S(1)}, u32[]{:S(2)}, u32[]{:S(2)}) collective-permute-start(f32[520,128]{1,0:T(8,128)S(1)} %get-tuple-element.132), channel_id=1, source_target_pairs={{1,13},{3,15},{5,1},{7,3},{9,5},{11,7},{13,9},{15,11},{17,29},{19,... | collective-permute-start | bytes 798728 | tf_op jit(solution)/shard_map/ppermute | solution.py:454
  144.5 8.7 %collective-permute-start.23 = (f32[520,128]{1,0:T(8,128)S(1)}, f32[520,128]{1,0:T(8,128)S(1)}, u32[]{:S(2)}, u32[]{:S(2)}) collective-permute-start(f32[520,128]{1,0:T(8,128)S(1)} %get-tuple-element.133), channel_id=1, source_target_pairs={{1,9},{3,11},{5,13},{7,15},{9,1},{11,3},{13,5},{15,7},{17,25},{19,... | collective-permute-start | bytes 798728 | tf_op jit(solution)/shard_map/ppermute | solution.py:454
  171.3 4.9 %collective-permute-start.26 = (f32[64,128]{1,0:T(8,128)S(1)}, f32[64,128]{1,0:T(8,128)S(1)}, u32[]{:S(2)}, u32[]{:S(2)}) collective-permute-start(f32[64,128]{1,0:T(8,128)S(1)} %shard_map.87.a), channel_id=1, source_target_pairs={{0,3},{1,2},{2,1},{3,0},{4,7},{5,6},{6,5},{7,4},{8,11},{9,10},{10,... | collective-permute-start | bytes 98312 | tf_op jit(solution)/shard_map/ppermute | solution.py:524
  171.4 4.8 %collective-permute-start.25 = (f32[64,128]{1,0:T(8,128)S(1)}, f32[64,128]{1,0:T(8,128)S(1)}, u32[]{:S(2)}, u32[]{:S(2)}) collective-permute-start(f32[64,128]{1,0:T(8,128)S(1)} %shard_map.87.a), channel_id=1, source_target_pairs={{0,2},{1,3},{2,0},{3,1},{4,6},{5,7},{6,4},{7,5},{8,10},{9,11},{10,... | collective-permute-start | bytes 98312 | tf_op jit(solution)/shard_map/ppermute | solution.py:524
  172.0 4.2 %collective-permute-start.24 = (f32[64,128]{1,0:T(8,128)S(1)}, f32[64,128]{1,0:T(8,128)S(1)}, u32[]{:S(2)}, u32[]{:S(2)}) collective-permute-start(f32[64,128]{1,0:T(8,128)S(1)} %shard_map.87.a), channel_id=1, source_target_pairs={{0,1},{1,0},{2,3},{3,2},{4,5},{5,4},{6,7},{7,6},{8,9},{9,8},{10,11... | collective-permute-start | bytes 98312 | tf_op jit(solution)/shard_map/ppermute | solution.py:524
  176.2 5.5 %collective-permute-start.29 = (f32[4,64,128]{2,1,0:T(8,128)S(1)}, f32[4,64,128]{2,1,0:T(8,128)S(1)}, u32[]{:S(2)}, u32[]{:S(2)}) collective-permute-start(f32[4,64,128]{2,1,0:T(8,128)S(1)} %shard_map.88.own), channel_id=1, source_target_pairs={{12,0},{13,1},{14,2},{15,3},{0,4},{1,5},{2,6},{3,7},{4,8},{5,9},{6... | collective-permute-start | bytes 393224 | tf_op jit(solution)/shard_map/ppermute | solution.py:526
  177.2 8.0 %collective-permute-start.28 = (f32[4,64,128]{2,1,0:T(8,128)S(1)}, f32[4,64,128]{2,1,0:T(8,128)S(1)}, u32[]{:S(2)}, u32[]{:S(2)}) collective-permute-start(f32[4,64,128]{2,1,0:T(8,128)S(1)} %shard_map.88.own), channel_id=1, source_target_pairs={{8,0},{9,1},{10,2},{11,3},{12,4},{13,5},{14,6},{15,7},{0,8},{1,9},... | collective-permute-start | bytes 393224 | tf_op jit(solution)/shard_map/ppermute | solution.py:526
  180.6 5.5 %collective-permute-start.27 = (f32[4,64,128]{2,1,0:T(8,128)S(1)}, f32[4,64,128]{2,1,0:T(8,128)S(1)}, u32[]{:S(2)}, u32[]{:S(2)}) collective-permute-start(f32[4,64,128]{2,1,0:T(8,128)S(1)} %shard_map.88.own), channel_id=1, source_target_pairs={{4,0},{5,1},{6,2},{7,3},{8,4},{9,5},{10,6},{11,7},{12,8},{13,9},{1... | collective-permute-start | bytes 393224 | tf_op jit(solution)/shard_map/ppermute | solution.py:526
where the time goes:
time: 188 us
  starting transfers between devices  67.4 us (36%)
  waiting for transfers between devices  63.8 us (34%)
  Pallas kernels  37.4 us (20%)
  blocking collectives  16.4 us (9%)
    all_to_all x1, waiting for transfers between devices, on_device(): slab = lax.all_to_all(parts, 'band', 0, 0, tiled=True)  36.3 us
    pallas_call x12, Pallas kernels, call(): pl.pallas_call(kernel, out_shape=outs[0] if single else outs, in_specs=sp...  31.2 us
    ppermute x15, starting transfers between devices, on_device(): lax.ppermute(came[i], 'band', [(j, band_at(j, move)) for j in range(16)])  28.1 us
    ppermute x6, waiting for transfers between devices, reduced_over_dom(): got = [lax.ppermute(v, 'dom', moves(*s)) for v, s in zip(sends, steps)]  18.7 us
    all_to_all x1, blocking collectives, on_device(): parts = lax.all_to_all(parts, 'band', 0, 0, tiled=True)  16.4 us
    all_to_all x1, starting transfers between devices, on_device(): slab = lax.all_to_all(parts, 'band', 0, 0, tiled=True)  10.4 us
    ppermute x6, starting transfers between devices, reduced_over_dom(): got = [lax.ppermute(v, 'dom', moves(*s)) for v, s in zip(sends, steps)]  10.3 us
    ppermute x1, starting transfers between devices, on_device(): mate = lax.ppermute(send, 'dom', [(i, i ^ 1) for i in range(16)])  7.01 us
  transfers between devices with their start and end apart: 31, of which 12 were waited for; matrix products, arithmetic and copies ran while one was open for 0% of the time, Pallas kernels for 9%

commit v1 on v0

--- a/solution.py
+++ b/solution.py
@@ -71,11 +71,14 @@
     two.wait()
 
 
-def edge_kernel(r, first, below):
+def plane_kernel(r, out):
+    out[...] = r[...]
+
+
+def edge_kernel(r, below):
     lane = lane_of((32, 128))
 
     def body(g, _):
-        first[g] = r[g, :64, :]
         acc = r[g, :32, :]
         for i in (1, 2, 4, 5, 6):
             at = i % 4 * 64 + i // 4 * 32
@@ -492,7 +495,16 @@
         if i:
             came[i] = lax.ppermute(came[i], "band", [(j, band_at(j, move)) for j in range(16)])
     back = [((i + 1) % 16, i) for i in range(16)]
-    first, below = call(edge_kernel, (slab,), [shape(16, bands, 128), shape(16, bands // 2, 128)], mib=4)
+    first = pl.pallas_call(
+        plane_kernel,
+        grid=(1,),
+        out_shape=shape(16, bands, 128),
+        in_specs=[pl.BlockSpec((16, bands, 128), lambda i: (0, 0, 0))],
+        out_specs=pl.BlockSpec((16, bands, 128), lambda i: (0, 0, 0)),
+        compiler_params=pltpu.CompilerParams(vmem_limit_bytes=4 * 1024 * 1024),
+        cost_estimate=pl.CostEstimate(flops=1000, bytes_accessed=2**20, transcendentals=0),
+    )(slab)
+    below = call(edge_kernel, (slab,), [shape(16, bands // 2, 128)], mib=4)
     ahead, above = lax.ppermute(first, "dom", back), lax.ppermute(below, "band", back)
     m = 16 * bands
     three, wide = shape(m, 384, dtype=BF16), shape(m, 512, dtype=BF16)

time: 188 us -> 186 us (0.989)
  Pallas kernels: 37.4 us -> 34.6 us
    pallas_call x12, Pallas kernels: 31.2 us -> 28.4 us  [call(): pl.pallas_call(kernel, out_shape=outs[0] if single else outs, in_specs=sp...]
  transfers between devices with their start and end apart: 31 -> 31, of which waited for: 12 -> 11; matrix products, arithmetic and copies ran while one was open for 0% -> 0% of each run, Pallas kernels for 9% -> 9%
where the time goes in v1:
time: 186 us; the launch traced here: 185 us
  starting transfers between devices  67.1 us (36%)
  waiting for transfers between devices  62.8 us (34%)
  Pallas kernels  34.6 us (19%)
  blocking collectives  17.7 us (10%)
    all_to_all x1, waiting for transfers between devices, on_device(): slab = lax.all_to_all(parts, 'band', 0, 0, tiled=True)  36.2 us
    pallas_call x12, Pallas kernels, call(): pl.pallas_call(kernel, out_shape=outs[0] if single else outs, in_specs=sp...  28.4 us
    ppermute x15, starting transfers between devices, on_device(): lax.ppermute(came[i], 'band', [(j, band_at(j, move)) for j in range(16)])  27.5 us
    ppermute x6, waiting for transfers between devices, reduced_over_dom(): got = [lax.ppermute(v, 'dom', moves(*s)) for v, s in zip(sends, steps)]  18.5 us
    all_to_all x1, blocking collectives, on_device(): parts = lax.all_to_all(parts, 'band', 0, 0, tiled=True)  17.7 us
    ppermute x6, starting transfers between devices, reduced_over_dom(): got = [lax.ppermute(v, 'dom', moves(*s)) for v, s in zip(sends, steps)]  10.5 us
    all_to_all x1, starting transfers between devices, on_device(): slab = lax.all_to_all(parts, 'band', 0, 0, tiled=True)  10.3 us
    ppermute x1, starting transfers between devices, on_device(): mate = lax.ppermute(send, 'dom', [(i, i ^ 1) for i in range(16)])  7.1 us
  transfers between devices with their start and end apart: 31, of which 11 were waited for; matrix products, arithmetic and copies ran while one was open for 0% of the time, Pallas kernels for 9%

profile of v1, /device:TPU:1, one launch (start us, length us, event | category | flops | bytes accessed | tf_op | source)
XLA Modules:
  0.0 184.8 jit_solution(13011419532564546259)
XLA Ops:
  0.6 6.2 %shard_map.77 = (f32[16,192,128]{2,1,0:T(8,128)}, f32[16,64,128]{2,1,0:T(8,128)}) custom-call(f32[4096,128]{1,0:T(8,128)} %bitcast.4), custom_call_target="tpu_custom_call" | custom-call | tf_op jit(solution)/shard_map/pallas_call | solution.py:469
  6.9 10.3 %all-to-all-start = ((f32[16,192,128]{2,1,0:T(8,128)}), f32[16,192,128]{2,1,0:T(8,128)S(1)}, u32[]{:S(2)}, u32[]{:S(2)}) async-start(f32[16,192,128]{2,1,0:T(8,128)} %get-tuple-element.66), calls=%async_computation | async-start | bytes 3145728 | tf_op jit(solution)/shard_map/all_to_all | solution.py:481
  17.3 36.2 %all-to-all-done.r = f32[16,192,128]{2,1,0:T(8,128)S(1)} async-done(((f32[16,192,128]{2,1,0:T(8,128)}), f32[16,192,128]{2,1,0:T(8,128)S(1)}, u32[]{:S(2)}, u32[]{:S(2)}) %all-to-all-start) | async-done | bytes 1572896 | tf_op jit(solution)/shard_map/all_to_all | solution.py:481
  53.6 2.7 %collective-permute-start = (f32[16,64,128]{2,1,0:T(8,128)S(1)}, f32[16,64,128]{2,1,0:T(8,128)S(1)}, u32[]{:S(2)}, u32[]{:S(2)}) collective-permute-start(f32[16,64,128]{2,1,0:T(8,128)S(1)} %shard_map.81), channel_id=1, source_target_pairs={{1,0},{2,1},{3,2},{4,3},{5,4},{6,5},{7,6},{8,7},{9,8},{10,9},{11,1... | collective-permute-start | bytes 1572872 | tf_op jit(solution)/shard_map/ppermute | solution.py:508
  56.4 1.7 copy-done.1
  58.0 7.6 %shard_map.79 = (f32[4,128]{1,0:T(4,128)S(1)}, f32[80,128]{1,0:T(8,128)S(1)}, f32[80,128]{1,0:T(8,128)S(1)}, f32[80,128]{1,0:T(8,128)S(1)}, f32[80,128]{1,0:T(8,...) custom-call(s32[2]{0:T(128)S(1)} %pad_add_fusion.ids, ...), custom_call_target="tpu_custom_call" | custom-call | flops 46153920 | bytes 5769240 | tf_op jit(solution)/shard_map/pallas_call | solution.py:425
  65.7 3.0 %collective-permute-start.2 = (f32[80,128]{1,0:T(8,128)S(1)}, f32[80,128]{1,0:T(8,128)S(1)}, u32[]{:S(2)}, u32[]{:S(2)}) collective-permute-start(f32[80,128]{1,0:T(8,128)S(1)} %get-tuple-element.77), channel_id=1, source_target_pairs={{0,64},{16,80},{32,96},{48,112},{64,0},{80,16},{96,32},{112,48},{1... | collective-permute-start | bytes 122888 | tf_op jit(solution)/shard_map/ppermute | solution.py:496
  68.7 2.2 %collective-permute-start.3 = (f32[80,128]{1,0:T(8,128)S(1)}, f32[80,128]{1,0:T(8,128)S(1)}, u32[]{:S(2)}, u32[]{:S(2)}) collective-permute-start(f32[80,128]{1,0:T(8,128)S(1)} %get-tuple-element.78), channel_id=1, source_target_pairs={{0,192},{16,208},{32,224},{48,240},{64,128},{80,144},{96,160},{112... | collective-permute-start | bytes 122888 | tf_op jit(solution)/shard_map/ppermute | solution.py:496
  70.9 3.2 %collective-permute-start.4 = (f32[80,128]{1,0:T(8,128)S(1)}, f32[80,128]{1,0:T(8,128)S(1)}, u32[]{:S(2)}, u32[]{:S(2)}) collective-permute-start(f32[80,128]{1,0:T(8,128)S(1)} %get-tuple-element.79), channel_id=1, source_target_pairs={{0,48},{16,64},{32,80},{48,96},{64,112},{80,0},{96,16},{112,32},{1... | collective-permute-start | bytes 122888 | tf_op jit(solution)/shard_map/ppermute | solution.py:496
  74.1 2.1 %collective-permute-start.5 = (f32[80,128]{1,0:T(8,128)S(1)}, f32[80,128]{1,0:T(8,128)S(1)}, u32[]{:S(2)}, u32[]{:S(2)}) collective-permute-start(f32[80,128]{1,0:T(8,128)S(1)} %get-tuple-element.80), channel_id=1, source_target_pairs={{0,176},{16,192},{32,208},{48,224},{64,240},{80,128},{96,144},{112... | collective-permute-start | bytes 122888 | tf_op jit(solution)/shard_map/ppermute | solution.py:496
  76.2 2.4 %collective-permute-start.6 = (f32[80,128]{1,0:T(8,128)S(1)}, f32[80,128]{1,0:T(8,128)S(1)}, u32[]{:S(2)}, u32[]{:S(2)}) collective-permute-start(f32[80,128]{1,0:T(8,128)S(1)} %get-tuple-element.81), channel_id=1, source_target_pairs={{0,80},{16,96},{32,112},{48,0},{64,16},{80,32},{96,48},{112,64},{1... | collective-permute-start | bytes 122888 | tf_op jit(solution)/shard_map/ppermute | solution.py:496
  78.6 2.1 %collective-permute-start.7 = (f32[80,128]{1,0:T(8,128)S(1)}, f32[80,128]{1,0:T(8,128)S(1)}, u32[]{:S(2)}, u32[]{:S(2)}) collective-permute-start(f32[80,128]{1,0:T(8,128)S(1)} %get-tuple-element.82), channel_id=1, source_target_pairs={{0,208},{16,224},{32,240},{48,128},{64,144},{80,160},{96,176},{112... | collective-permute-start | bytes 122888 | tf_op jit(solution)/shard_map/ppermute | solution.py:496
  80.8 0.6 collective-permute-start.8
  81.4 1.2 collective-permute-done.5.refs_4_
  82.6 2.5 %collective-permute-start.9 = (f32[80,128]{1,0:T(8,128)S(1)}, f32[80,128]{1,0:T(8,128)S(1)}, u32[]{:S(2)}, u32[]{:S(2)}) collective-permute-start(f32[80,128]{1,0:T(8,128)S(1)} %get-tuple-element.84), channel_id=1, source_target_pairs={{0,160},{16,176},{32,192},{48,208},{64,224},{80,240},{96,128},{112... | collective-permute-start | bytes 122888 | tf_op jit(solution)/shard_map/ppermute | solution.py:496
  85.1 0.9 collective-permute-start.10
  86.0 2.8 %collective-permute-start.11 = (f32[80,128]{1,0:T(8,128)S(1)}, f32[80,128]{1,0:T(8,128)S(1)}, u32[]{:S(2)}, u32[]{:S(2)}) collective-permute-start(f32[80,128]{1,0:T(8,128)S(1)} %get-tuple-element.86), channel_id=1, source_target_pairs={{0,224},{16,240},{32,128},{48,144},{64,160},{80,176},{96,192},{112... | collective-permute-start | bytes 122888 | tf_op jit(solution)/shard_map/ppermute | solution.py:496
  88.8 0.8 collective-permute-start.12
  90.0 1.4 shard_map.82
  91.5 2.9 %collective-permute-start.14 = (f32[80,128]{1,0:T(8,128)S(1)}, f32[80,128]{1,0:T(8,128)S(1)}, u32[]{:S(2)}, u32[]{:S(2)}) collective-permute-start(f32[80,128]{1,0:T(8,128)S(1)} %get-tuple-element.89), channel_id=1, source_target_pairs={{0,112},{16,0},{32,16},{48,32},{64,48},{80,64},{96,80},{112,96},{1... | collective-permute-start | bytes 122888 | tf_op jit(solution)/shard_map/ppermute | solution.py:496
  94.3 1.2 collective-permute-start.15
  95.8 1.0 collective-permute-start.1
  96.8 4.1 %shard_map.80 = (bf16[1024,384]{1,0:T(8,128)(2,1)S(1)}, bf16[1024,384]{1,0:T(8,128)(2,1)S(1)}, f32[1024,384]{1,0:T(8,128)S(1)}, f32[2,3,256,256]{3,2,1,0:T(8,128)S(1)}, f32[512,512]{1,0:T(8,128)S(1)}) custom-call(f32[16,192,128]{2,1,0:T(8,128)S(1)} %all-to-all-done.r, f32[4,128]{1,0:T(4,128)S(1)} %get-tuple-element.73.pot), custom_call_target="tpu_custom_call" | custom-call | flops 3221225472 | bytes 7342080 | tf_op jit(solution)/shard_map/pallas_call | solution.py:425
  101.1 6.9 %shard_map.83 = (f32[8,520,128]{2,1,0:T(8,128)S(1)}, bf16[1024,512]{1,0:T(8,128)(2,1)S(1)}, bf16[1024,512]{1,0:T(8,128)(2,1)S(1)}, bf16[1024,512]{1,0:T(8,128)(2...) custom-call(s32[2]{0:T(128)S(1)} %pad_add_fusion.ids, ...), custom_call_target="tpu_custom_call" | custom-call | flops 3221225472 | bytes 13731848 | tf_op jit(solution)/shard_map/pallas_call | solution.py:425
  108.0 7.1 %collective-permute-start.17 = (f32[8,520,128]{2,1,0:T(8,128)S(1)}, f32[8,520,128]{2,1,0:T(8,128)S(1)}, u32[]{:S(2)}, u32[]{:S(2)}) collective-permute-start(f32[8,520,128]{2,1,0:T(8,128)S(1)} %get-tuple-element.121), channel_id=1, source_target_pairs={{0,1},{1,0},{2,3},{3,2},{4,5},{5,4},{6,7},{7,6},{8,9},{9,8},{10,11... | collective-permute-start | bytes 6389768 | tf_op jit(solution)/shard_map/ppermute | solution.py:531
  115.1 3.3 %shard_map.84.keep = f32[8,520,128]{2,1,0:T(8,128)S(1)} custom-call(s32[2]{0:T(128)S(1)} %pad_add_fusion.ids, bf16[1024,512]{1,0:T(8,128)(2,1)S(1)} %get-tuple-element.114.ph, bf16[1024,512]{1,0:T(8,128)(2,1)S(1)} %get-tuple-element.115.lo, bf16[1024,512]{1,0:T(8,128)(2,1)S(1)} %get-tuple-element.116.ah, bf16[1024,512]{1,0:T(8,128)(2,1)S(1)} %get-tuple-element.117.al, ...), custom_call_target="tpu_custom_call" | custom-call | flops 3221225472 | bytes 9142280 | tf_op jit(solution)/shard_map/pallas_call | solution.py:425
  118.9 0.9 shard_map.85
  119.9 1.7 collective-permute-start.18
  121.5 1.4 collective-permute-start.19
  122.9 0.7 collective-permute-start.20
  123.6 6.0 %collective-permute-done.18.r1 = f32[2,520,128]{2,1,0:T(8,128)S(1)} collective-permute-done((f32[2,520,128]{2,1,0:T(8,128)S(1)}, f32[2,520,128]{2,1,0:T(8,128)S(1)}, u32[]{:S(2)}, u32[]{:S(2)}) %collective-permute-start.18) | collective-permute-done | bytes 532512 | tf_op jit(solution)/shard_map/ppermute | solution.py:454
  129.6 6.0 %collective-permute-done.19.r2 = f32[2,520,128]{2,1,0:T(8,128)S(1)} collective-permute-done((f32[2,520,128]{2,1,0:T(8,128)S(1)}, f32[2,520,128]{2,1,0:T(8,128)S(1)}, u32[]{:S(2)}, u32[]{:S(2)}) %collective-permute-start.19) | collective-permute-done | bytes 532512 | tf_op jit(solution)/shard_map/ppermute | solution.py:454
  135.6 0.7 shard_map.86
  136.4 4.6 %collective-permute-start.22 = (f32[520,128]{1,0:T(8,128)S(1)}, f32[520,128]{1,0:T(8,128)S(1)}, u32[]{:S(2)}, u32[]{:S(2)}) collective-permute-start(f32[520,128]{1,0:T(8,128)S(1)} %get-tuple-element.128), channel_id=1, source_target_pairs={{1,13},{3,15},{5,1},{7,3},{9,5},{11,7},{13,9},{15,11},{17,29},{19,... | collective-permute-start | bytes 798728 | tf_op jit(solution)/shard_map/ppermute | solution.py:457
  140.9 2.1 %collective-permute-start.23 = (f32[520,128]{1,0:T(8,128)S(1)}, f32[520,128]{1,0:T(8,128)S(1)}, u32[]{:S(2)}, u32[]{:S(2)}) collective-permute-start(f32[520,128]{1,0:T(8,128)S(1)} %get-tuple-element.129), channel_id=1, source_target_pairs={{1,9},{3,11},{5,13},{7,15},{9,1},{11,3},{13,5},{15,7},{17,25},{19,... | collective-permute-start | bytes 798728 | tf_op jit(solution)/shard_map/ppermute | solution.py:457
  143.1 4.0 %collective-permute-done.22.r2 = f32[520,128]{1,0:T(8,128)S(1)} collective-permute-done((f32[520,128]{1,0:T(8,128)S(1)}, f32[520,128]{1,0:T(8,128)S(1)}, u32[]{:S(2)}, u32[]{:S(2)}) %collective-permute-start.22) | collective-permute-done | bytes 266272 | tf_op jit(solution)/shard_map/ppermute | solution.py:457
  147.1 2.5 %collective-permute-done.23.r3 = f32[520,128]{1,0:T(8,128)S(1)} collective-permute-done((f32[520,128]{1,0:T(8,128)S(1)}, f32[520,128]{1,0:T(8,128)S(1)}, u32[]{:S(2)}, u32[]{:S(2)}) %collective-permute-start.23) | collective-permute-done | bytes 266272 | tf_op jit(solution)/shard_map/ppermute | solution.py:457
  149.6 1.0 shard_map.87
  150.6 17.7 %all_to_all.10.parts = f32[16,64,128]{2,1,0:T(8,128)S(1)} all-to-all(f32[16,64,128]{2,1,0:T(8,128)S(1)} %shard_map.87), channel_id=1, replica_groups=mesh['band'=16,'dom'=16] {'band'}, dimensions={0} | all-to-all | bytes 1048576 | tf_op jit(solution)/shard_map/all_to_all | solution.py:534
  168.3 0.7 shard_map.88.a
  169.1 1.3 collective-permute-start.25
  170.4 2.3 %collective-permute-start.24 = (f32[64,128]{1,0:T(8,128)S(1)}, f32[64,128]{1,0:T(8,128)S(1)}, u32[]{:S(2)}, u32[]{:S(2)}) collective-permute-start(f32[64,128]{1,0:T(8,128)S(1)} %shard_map.88.a), channel_id=1, source_target_pairs={{0,1},{1,0},{2,3},{3,2},{4,5},{5,4},{6,7},{7,6},{8,9},{9,8},{10,11... | collective-permute-start | bytes 98312 | tf_op jit(solution)/shard_map/ppermute | solution.py:536
  172.7 1.2 collective-permute-done.26.d
  173.9 0.9 collective-permute-start.29
  174.8 3.4 %collective-permute-start.28 = (f32[4,64,128]{2,1,0:T(8,128)S(1)}, f32[4,64,128]{2,1,0:T(8,128)S(1)}, u32[]{:S(2)}, u32[]{:S(2)}) collective-permute-start(f32[4,64,128]{2,1,0:T(8,128)S(1)} %shard_map.89.own), channel_id=1, source_target_pairs={{8,0},{9,1},{10,2},{11,3},{12,4},{13,5},{14,6},{15,7},{0,8},{1,9},... | collective-permute-start | bytes 393224 | tf_op jit(solution)/shard_map/ppermute | solution.py:538
  178.2 1.2 collective-permute-done.29.r3
  179.4 3.8 %collective-permute-done.28.r2 = f32[4,64,128]{2,1,0:T(8,128)S(1)} collective-permute-done((f32[4,64,128]{2,1,0:T(8,128)S(1)}, f32[4,64,128]{2,1,0:T(8,128)S(1)}, u32[]{:S(2)}, u32[]{:S(2)}) %collective-permute-start.28) | collective-permute-done | bytes 131104 | tf_op jit(solution)/shard_map/ppermute | solution.py:538
  183.3 1.6 shard_map.90
  (46 shorter events, 1.9 us)
Async XLA Ops:
  6.8 10.3 %copy-start.5 = (f32[4,18,18]{2,0,1:T(4,128)S(1)}, f32[4,18,18]{2,0,1:T(4,128)}, u32[]{:S(2)}) copy-start(f32[4,18,18]{2,0,1:T(4,128)} %param.9) | copy-start | bytes 15556
  6.8 10.3 %copy-start.6 = (f32[4,18,18]{2,0,1:T(4,128)S(1)}, f32[4,18,18]{2,0,1:T(4,128)}, u32[]{:S(2)}) copy-start(f32[4,18,18]{2,0,1:T(4,128)} %param.10) | copy-start | bytes 15556
  6.8 49.5 %copy-start.2 = (f32[16,64,128]{2,1,0:T(8,128)S(1)}, f32[16,64,128]{2,1,0:T(8,128)}, u32[]{:S(2)}) copy-start(f32[16,64,128]{2,1,0:T(8,128)} %get-tuple-element.72.last) | copy-start | bytes 1572868
  6.9 49.5 %copy-start.3 = (f32[4,16,128]{2,1,0:T(8,128)S(1)}, f32[4,16,128]{2,1,0:T(8,128)}, u32[]{:S(2)}) copy-start(f32[4,16,128]{2,1,0:T(8,128)} %potential) | copy-start | bytes 98308
  6.9 49.5 %copy-start.4 = (s32[4]{0:T(128)S(1)}, s32[4]{0:T(128)}, u32[]{:S(2)}) copy-start(s32[4]{0:T(128)} %count.1) | copy-start | bytes 52
  6.9 46.6 %all-to-all-start = ((f32[16,192,128]{2,1,0:T(8,128)}), f32[16,192,128]{2,1,0:T(8,128)S(1)}, u32[]{:S(2)}, u32[]{:S(2)}) async-start(f32[16,192,128]{2,1,0:T(8,128)} %get-tuple-element.66), calls=%async_computation | async-start | bytes 3145728 | tf_op jit(solution)/shard_map/all_to_all | solution.py:481
  53.5 2.9 %copy-start = (f32[64,4,16,128]{3,2,1,0:T(8,128)S(1)}, f32[64,4,16,128]{3,2,1,0:T(8,128)}, u32[]{:S(2)}) copy-start(f32[64,4,16,128]{3,2,1,0:T(8,128)} %param.6) | copy-start | bytes 6291460
  53.6 47.5 %collective-permute-start = (f32[16,64,128]{2,1,0:T(8,128)S(1)}, f32[16,64,128]{2,1,0:T(8,128)S(1)}, u32[]{:S(2)}, u32[]{:S(2)}) collective-permute-start(f32[16,64,128]{2,1,0:T(8,128)S(1)} %shard_map.81), channel_id=1, source_target_pairs={{1,0},{2,1},{3,2},{4,3},{5,4},{6,5},{7,6},{8,7},{9,8},{10,9},{11,1... | collective-permute-start | bytes 1572872 | tf_op jit(solution)/shard_map/ppermute | solution.py:508
  56.4 1.7 copy-start.1
  65.7 10.5 %collective-permute-start.2 = (f32[80,128]{1,0:T(8,128)S(1)}, f32[80,128]{1,0:T(8,128)S(1)}, u32[]{:S(2)}, u32[]{:S(2)}) collective-permute-start(f32[80,128]{1,0:T(8,128)S(1)} %get-tuple-element.77), channel_id=1, source_target_pairs={{0,64},{16,80},{32,96},{48,112},{64,0},{80,16},{96,32},{112,48},{1... | collective-permute-start | bytes 122888 | tf_op jit(solution)/shard_map/ppermute | solution.py:496
  68.7 9.9 %collective-permute-start.3 = (f32[80,128]{1,0:T(8,128)S(1)}, f32[80,128]{1,0:T(8,128)S(1)}, u32[]{:S(2)}, u32[]{:S(2)}) collective-permute-start(f32[80,128]{1,0:T(8,128)S(1)} %get-tuple-element.78), channel_id=1, source_target_pairs={{0,192},{16,208},{32,224},{48,240},{64,128},{80,144},{96,160},{112... | collective-permute-start | bytes 122888 | tf_op jit(solution)/shard_map/ppermute | solution.py:496
  70.9 9.9 %collective-permute-start.4 = (f32[80,128]{1,0:T(8,128)S(1)}, f32[80,128]{1,0:T(8,128)S(1)}, u32[]{:S(2)}, u32[]{:S(2)}) collective-permute-start(f32[80,128]{1,0:T(8,128)S(1)} %get-tuple-element.79), channel_id=1, source_target_pairs={{0,48},{16,64},{32,80},{48,96},{64,112},{80,0},{96,16},{112,32},{1... | collective-permute-start | bytes 122888 | tf_op jit(solution)/shard_map/ppermute | solution.py:496
  74.1 8.5 %collective-permute-start.5 = (f32[80,128]{1,0:T(8,128)S(1)}, f32[80,128]{1,0:T(8,128)S(1)}, u32[]{:S(2)}, u32[]{:S(2)}) collective-permute-start(f32[80,128]{1,0:T(8,128)S(1)} %get-tuple-element.80), channel_id=1, source_target_pairs={{0,176},{16,192},{32,208},{48,224},{64,240},{80,128},{96,144},{112... | collective-permute-start | bytes 122888 | tf_op jit(solution)/shard_map/ppermute | solution.py:496
  76.2 8.9 %collective-permute-start.6 = (f32[80,128]{1,0:T(8,128)S(1)}, f32[80,128]{1,0:T(8,128)S(1)}, u32[]{:S(2)}, u32[]{:S(2)}) collective-permute-start(f32[80,128]{1,0:T(8,128)S(1)} %get-tuple-element.81), channel_id=1, source_target_pairs={{0,80},{16,96},{32,112},{48,0},{64,16},{80,32},{96,48},{112,64},{1... | collective-permute-start | bytes 122888 | tf_op jit(solution)/shard_map/ppermute | solution.py:496
  78.6 7.3 %collective-permute-start.7 = (f32[80,128]{1,0:T(8,128)S(1)}, f32[80,128]{1,0:T(8,128)S(1)}, u32[]{:S(2)}, u32[]{:S(2)}) collective-permute-start(f32[80,128]{1,0:T(8,128)S(1)} %get-tuple-element.82), channel_id=1, source_target_pairs={{0,208},{16,224},{32,240},{48,128},{64,144},{80,160},{96,176},{112... | collective-permute-start | bytes 122888 | tf_op jit(solution)/shard_map/ppermute | solution.py:496
  80.8 8.0 %collective-permute-start.8 = (f32[80,128]{1,0:T(8,128)S(1)}, f32[80,128]{1,0:T(8,128)S(1)}, u32[]{:S(2)}, u32[]{:S(2)}) collective-permute-start(f32[80,128]{1,0:T(8,128)S(1)} %get-tuple-element.83), channel_id=1, source_target_pairs={{0,32},{16,48},{32,64},{48,80},{64,96},{80,112},{96,0},{112,16},{1... | collective-permute-start | bytes 122888 | tf_op jit(solution)/shard_map/ppermute | solution.py:496
  82.6 7.0 %collective-permute-start.9 = (f32[80,128]{1,0:T(8,128)S(1)}, f32[80,128]{1,0:T(8,128)S(1)}, u32[]{:S(2)}, u32[]{:S(2)}) collective-permute-start(f32[80,128]{1,0:T(8,128)S(1)} %get-tuple-element.84), channel_id=1, source_target_pairs={{0,160},{16,176},{32,192},{48,208},{64,224},{80,240},{96,128},{112... | collective-permute-start | bytes 122888 | tf_op jit(solution)/shard_map/ppermute | solution.py:496
  85.1 6.4 %collective-permute-start.10 = (f32[80,128]{1,0:T(8,128)S(1)}, f32[80,128]{1,0:T(8,128)S(1)}, u32[]{:S(2)}, u32[]{:S(2)}) collective-permute-start(f32[80,128]{1,0:T(8,128)S(1)} %get-tuple-element.85), channel_id=1, source_target_pairs={{0,96},{16,112},{32,0},{48,16},{64,32},{80,48},{96,64},{112,80},{1... | collective-permute-start | bytes 122888 | tf_op jit(solution)/shard_map/ppermute | solution.py:496
  86.0 8.3 %collective-permute-start.11 = (f32[80,128]{1,0:T(8,128)S(1)}, f32[80,128]{1,0:T(8,128)S(1)}, u32[]{:S(2)}, u32[]{:S(2)}) collective-permute-start(f32[80,128]{1,0:T(8,128)S(1)} %get-tuple-element.86), channel_id=1, source_target_pairs={{0,224},{16,240},{32,128},{48,144},{64,160},{80,176},{96,192},{112... | collective-permute-start | bytes 122888 | tf_op jit(solution)/shard_map/ppermute | solution.py:496
  88.8 6.7 %collective-permute-start.12 = (f32[80,128]{1,0:T(8,128)S(1)}, f32[80,128]{1,0:T(8,128)S(1)}, u32[]{:S(2)}, u32[]{:S(2)}) collective-permute-start(f32[80,128]{1,0:T(8,128)S(1)} %get-tuple-element.87), channel_id=1, source_target_pairs={{0,16},{16,32},{32,48},{48,64},{64,80},{80,96},{96,112},{112,0},{1... | collective-permute-start | bytes 122888 | tf_op jit(solution)/shard_map/ppermute | solution.py:496
  89.6 6.2 %collective-permute-start.13 = (f32[80,128]{1,0:T(8,128)S(1)}, f32[80,128]{1,0:T(8,128)S(1)}, u32[]{:S(2)}, u32[]{:S(2)}) collective-permute-start(f32[80,128]{1,0:T(8,128)S(1)} %get-tuple-element.88), channel_id=1, source_target_pairs={{0,144},{16,160},{32,176},{48,192},{64,208},{80,224},{96,240},{112... | collective-permute-start | bytes 122888 | tf_op jit(solution)/shard_map/ppermute | solution.py:496
  91.5 9.5 %collective-permute-start.14 = (f32[80,128]{1,0:T(8,128)S(1)}, f32[80,128]{1,0:T(8,128)S(1)}, u32[]{:S(2)}, u32[]{:S(2)}) collective-permute-start(f32[80,128]{1,0:T(8,128)S(1)} %get-tuple-element.89), channel_id=1, source_target_pairs={{0,112},{16,0},{32,16},{48,32},{64,48},{80,64},{96,80},{112,96},{1... | collective-permute-start | bytes 122888 | tf_op jit(solution)/shard_map/ppermute | solution.py:496
  94.3 6.6 %collective-permute-start.15 = (f32[80,128]{1,0:T(8,128)S(1)}, f32[80,128]{1,0:T(8,128)S(1)}, u32[]{:S(2)}, u32[]{:S(2)}) collective-permute-start(f32[80,128]{1,0:T(8,128)S(1)} %get-tuple-element.90), channel_id=1, source_target_pairs={{0,240},{16,128},{32,144},{48,160},{64,176},{80,192},{96,208},{112... | collective-permute-start | bytes 122888 | tf_op jit(solution)/shard_map/ppermute | solution.py:496
  95.5 5.5 %collective-permute-start.16 = (f32[80,128]{1,0:T(8,128)S(1)}, f32[80,128]{1,0:T(8,128)S(1)}, u32[]{:S(2)}, u32[]{:S(2)}) collective-permute-start(f32[80,128]{1,0:T(8,128)S(1)} %get-tuple-element.91), channel_id=1, source_target_pairs={{0,128},{16,144},{32,160},{48,176},{64,192},{80,208},{96,224},{112... | collective-permute-start | bytes 122888 | tf_op jit(solution)/shard_map/ppermute | solution.py:496
  95.8 5.2 %collective-permute-start.1 = (f32[16,32,128]{2,1,0:T(8,128)S(1)}, f32[16,32,128]{2,1,0:T(8,128)S(1)}, u32[]{:S(2)}, u32[]{:S(2)}) collective-permute-start(f32[16,32,128]{2,1,0:T(8,128)S(1)} %shard_map.82), channel_id=1, source_target_pairs={{16,0},{32,16},{48,32},{64,48},{80,64},{96,80},{112,96},{128,112},... | collective-permute-start | bytes 786440 | tf_op jit(solution)/shard_map/ppermute | solution.py:508
  108.0 10.9 %collective-permute-start.17 = (f32[8,520,128]{2,1,0:T(8,128)S(1)}, f32[8,520,128]{2,1,0:T(8,128)S(1)}, u32[]{:S(2)}, u32[]{:S(2)}) collective-permute-start(f32[8,520,128]{2,1,0:T(8,128)S(1)} %get-tuple-element.121), channel_id=1, source_target_pairs={{0,1},{1,0},{2,3},{3,2},{4,5},{5,4},{6,7},{7,6},{8,9},{9,8},{10,11... | collective-permute-start | bytes 6389768 | tf_op jit(solution)/shard_map/ppermute | solution.py:531
  119.9 9.7 %collective-permute-start.18 = (f32[2,520,128]{2,1,0:T(8,128)S(1)}, f32[2,520,128]{2,1,0:T(8,128)S(1)}, u32[]{:S(2)}, u32[]{:S(2)}) collective-permute-start(f32[2,520,128]{2,1,0:T(8,128)S(1)} %get-tuple-element.123), channel_id=1, source_target_pairs={{0,4},{1,3},{2,6},{3,1},{4,8},{5,7},{6,10},{7,5},{8,12},{9,11},{10... | collective-permute-start | bytes 1597448 | tf_op jit(solution)/shard_map/ppermute | solution.py:454
  121.5 14.0 %collective-permute-start.19 = (f32[2,520,128]{2,1,0:T(8,128)S(1)}, f32[2,520,128]{2,1,0:T(8,128)S(1)}, u32[]{:S(2)}, u32[]{:S(2)}) collective-permute-start(f32[2,520,128]{2,1,0:T(8,128)S(1)} %get-tuple-element.124), channel_id=1, source_target_pairs={{0,12},{1,3},{2,14},{3,1},{4,0},{5,7},{6,2},{7,5},{8,4},{9,11},{10... | collective-permute-start | bytes 1597448 | tf_op jit(solution)/shard_map/ppermute | solution.py:454
  122.9 12.7 %collective-permute-start.20 = (f32[2,520,128]{2,1,0:T(8,128)S(1)}, f32[2,520,128]{2,1,0:T(8,128)S(1)}, u32[]{:S(2)}, u32[]{:S(2)}) collective-permute-start(f32[2,520,128]{2,1,0:T(8,128)S(1)} %get-tuple-element.125), channel_id=1, source_target_pairs={{0,8},{2,10},{4,12},{6,14},{8,0},{10,2},{12,4},{14,6},{16,24},{18,... | collective-permute-start | bytes 1597448 | tf_op jit(solution)/shard_map/ppermute | solution.py:454
  136.3 6.8 %collective-permute-start.21 = (f32[520,128]{1,0:T(8,128)S(1)}, f32[520,128]{1,0:T(8,128)S(1)}, u32[]{:S(2)}, u32[]{:S(2)}) collective-permute-start(f32[520,128]{1,0:T(8,128)S(1)} %get-tuple-element.127), channel_id=1, source_target_pairs={{0,2},{1,5},{2,0},{3,7},{4,6},{5,9},{6,4},{7,11},{8,10},{9,13},{10... | collective-permute-start | bytes 798728 | tf_op jit(solution)/shard_map/ppermute | solution.py:457
  136.4 10.8 %collective-permute-start.22 = (f32[520,128]{1,0:T(8,128)S(1)}, f32[520,128]{1,0:T(8,128)S(1)}, u32[]{:S(2)}, u32[]{:S(2)}) collective-permute-start(f32[520,128]{1,0:T(8,128)S(1)} %get-tuple-element.128), channel_id=1, source_target_pairs={{1,13},{3,15},{5,1},{7,3},{9,5},{11,7},{13,9},{15,11},{17,29},{19,... | collective-permute-start | bytes 798728 | tf_op jit(solution)/shard_map/ppermute | solution.py:457
  140.9 8.7 %collective-permute-start.23 = (f32[520,128]{1,0:T(8,128)S(1)}, f32[520,128]{1,0:T(8,128)S(1)}, u32[]{:S(2)}, u32[]{:S(2)}) collective-permute-start(f32[520,128]{1,0:T(8,128)S(1)} %get-tuple-element.129), channel_id=1, source_target_pairs={{1,9},{3,11},{5,13},{7,15},{9,1},{11,3},{13,5},{15,7},{17,25},{19,... | collective-permute-start | bytes 798728 | tf_op jit(solution)/shard_map/ppermute | solution.py:457
  169.0 4.9 %collective-permute-start.26 = (f32[64,128]{1,0:T(8,128)S(1)}, f32[64,128]{1,0:T(8,128)S(1)}, u32[]{:S(2)}, u32[]{:S(2)}) collective-permute-start(f32[64,128]{1,0:T(8,128)S(1)} %shard_map.88.a), channel_id=1, source_target_pairs={{0,3},{1,2},{2,1},{3,0},{4,7},{5,6},{6,5},{7,4},{8,11},{9,10},{10,... | collective-permute-start | bytes 98312 | tf_op jit(solution)/shard_map/ppermute | solution.py:536
  169.1 4.8 %collective-permute-start.25 = (f32[64,128]{1,0:T(8,128)S(1)}, f32[64,128]{1,0:T(8,128)S(1)}, u32[]{:S(2)}, u32[]{:S(2)}) collective-permute-start(f32[64,128]{1,0:T(8,128)S(1)} %shard_map.88.a), channel_id=1, source_target_pairs={{0,2},{1,3},{2,0},{3,1},{4,6},{5,7},{6,4},{7,5},{8,10},{9,11},{10,... | collective-permute-start | bytes 98312 | tf_op jit(solution)/shard_map/ppermute | solution.py:536
  170.4 3.5 %collective-permute-start.24 = (f32[64,128]{1,0:T(8,128)S(1)}, f32[64,128]{1,0:T(8,128)S(1)}, u32[]{:S(2)}, u32[]{:S(2)}) collective-permute-start(f32[64,128]{1,0:T(8,128)S(1)} %shard_map.88.a), channel_id=1, source_target_pairs={{0,1},{1,0},{2,3},{3,2},{4,5},{5,4},{6,7},{7,6},{8,9},{9,8},{10,11... | collective-permute-start | bytes 98312 | tf_op jit(solution)/shard_map/ppermute | solution.py:536
  173.9 5.5 %collective-permute-start.29 = (f32[4,64,128]{2,1,0:T(8,128)S(1)}, f32[4,64,128]{2,1,0:T(8,128)S(1)}, u32[]{:S(2)}, u32[]{:S(2)}) collective-permute-start(f32[4,64,128]{2,1,0:T(8,128)S(1)} %shard_map.89.own), channel_id=1, source_target_pairs={{12,0},{13,1},{14,2},{15,3},{0,4},{1,5},{2,6},{3,7},{4,8},{5,9},{6... | collective-permute-start | bytes 393224 | tf_op jit(solution)/shard_map/ppermute | solution.py:538
  174.8 8.4 %collective-permute-start.28 = (f32[4,64,128]{2,1,0:T(8,128)S(1)}, f32[4,64,128]{2,1,0:T(8,128)S(1)}, u32[]{:S(2)}, u32[]{:S(2)}) collective-permute-start(f32[4,64,128]{2,1,0:T(8,128)S(1)} %shard_map.89.own), channel_id=1, source_target_pairs={{8,0},{9,1},{10,2},{11,3},{12,4},{13,5},{14,6},{15,7},{0,8},{1,9},... | collective-permute-start | bytes 393224 | tf_op jit(solution)/shard_map/ppermute | solution.py:538
  178.2 5.0 %collective-permute-start.27 = (f32[4,64,128]{2,1,0:T(8,128)S(1)}, f32[4,64,128]{2,1,0:T(8,128)S(1)}, u32[]{:S(2)}, u32[]{:S(2)}) collective-permute-start(f32[4,64,128]{2,1,0:T(8,128)S(1)} %shard_map.89.own), channel_id=1, source_target_pairs={{4,0},{5,1},{6,2},{7,3},{8,4},{9,5},{10,6},{11,7},{12,8},{13,9},{1... | collective-permute-start | bytes 393224 | tf_op jit(solution)/shard_map/ppermute | solution.py:538

commit v2 on v1

--- a/solution.py
+++ b/solution.py
@@ -206,8 +206,7 @@
             co[i : i + 256, j : j + 256] = corr(512 + i, j)
 
 
-def gram(which, ah, al, ph, lo, er, eh, es, ce, co, out, c, on):
-    volume = 1.0 / (512 * 256)
+def gram(which, ah, al, ph, lo, er, eh, ce, co, out, c, on):
     low = lane_of((64, 128)) < 64
 
     def ham(i, j):
@@ -215,11 +214,6 @@
         acc = dot(ph[i, :], ah[j, :]) + dot(ph[i, :], al[j, :]) + dot(lo[i, :], ah[j, :])
         acc += dot(ah[i, :], ph[j, :]) + dot(al[i, :], ph[j, :]) + dot(ah[i, :], lo[j, :])
         return acc + slots(eh, er, i, j)
-
-    def corr(v, i, j):
-        i, j, x = slice(i, i + 256), slice(j, j + 256), slice(384, 512)
-        acc = dot(ah[i, x], ah[j, x]) + dot(ah[i, x], al[j, x]) + dot(al[i, x], ah[j, x])
-        return v + acc * volume + slots(es, er, i, j)
 
     def tiles(e, f, t, get):
         for j in range(4):
@@ -236,9 +230,9 @@
         for q in range(2):
             at = q * 512
             c[q, :256, 256:] = ham(at, at + 256)
-            c[q, 256:, :256] = corr(ce[q, 1], at + 256, at)
+            c[q, 256:, :256] = ce[q, 1]
             for n in range(2):
-                here, own = slice(n * 256, n * 256 + 256), corr(ce[q, 2 * n], at + n * 256, at + n * 256)
+                here, own = slice(n * 256, n * 256 + 256), ce[q, 2 * n]
                 c[q, here, here] = jnp.where(row <= col, ham(at + n * 256, at + n * 256), own)
                 diagonal = jnp.sum(jnp.where(row == col, own, jnp.zeros_like(own)), axis=0, keepdims=True)
                 on[q, n] = jnp.broadcast_to(diagonal, (8, 256))
@@ -259,15 +253,14 @@
         for i in (0, 256):
             for j in (0, 256):
                 c[0, i : i + 256, j : j + 256] = ham(i, 512 + j)
-                c[1, i : i + 256, j : j + 256] = corr(co[i : i + 256, j : j + 256], 512 + i, j)
         for e in range(8):
             tiles(e, e, 0, lambda m, n: c[0, m * 64 : m * 64 + 64, n * 128 : n * 128 + 128])
-            tiles(e, e, 4, lambda m, n: c[1, m * 64 : m * 64 + 64, n * 128 : n * 128 + 128])
+            tiles(e, e, 4, lambda m, n: co[m * 64 : m * 64 + 64, n * 128 : n * 128 + 128])
             out[e, 512:, :] = jnp.zeros((8, 128), F32)
 
 
-def send_kernel(ids, part, xh, zh, pot, th, tl, ce, co, *refs):
-    came, (out, ph, lo, ah, al, er, eh, es, c, on, last, cc) = refs[:16], refs[16:]
+def fourth_kernel(ids, pot, three, th, tl, fe, fo, *refs):
+    came, (ah, al, part, er, eh, es, ce, co, last, cc) = refs[:16], refs[16:]
     volume = 1.0 / (512 * 256)
     lane = lane_of((64, 128))
     for m, v in zip(MOVES, came):
@@ -287,31 +280,52 @@
 
     def prepare(g, _):
         to = pl.ds(pl.multiple_of(place(g) * 64, 64), 64)
-        two = zh[g]
-        ext = jnp.concatenate([two, turn(two, -4)], axis=0)
-        end = lane % 8 == 7
         p = last[g, 8:, :]
         ah[to, :384], al[to, :384] = th[to, :], tl[to, :]
         ah[to, 384:], al[to, 384:] = split(p)
-        for x in range(3):
-            cols = slice(x * 128, (x + 1) * 128)
-            beside = jnp.where(end, turn(ext, 7 - x), jnp.zeros((64, 128), F32))
-            if x == 2:
-                beside = beside + p
-            ph[to, cols], lo[to, cols] = split((part[to, cols] - 0.5 * beside) * volume)
+        part[to, :256] = three[to, :256]
+        part[to, 256:384] = three[to, 256:] - 0.5 * p
         after = last[g, :8, :]
         after = jnp.concatenate([turn(after, 7 - i) for i in range(8)], axis=0)
-        beside = xh[g] + turn(p, -8) + jnp.where(end, after, turn(p, -1))
-        phi = (1.5 + 0.5 * pot[3:4, :]) * p - 0.5 * beside
-        ph[to, 384:], lo[to, 384:] = split(phi * volume)
+        beside = turn(p, -8) + jnp.where(lane % 8 == 7, after, turn(p, -1))
+        part[to, 384:] = (1.5 + 0.5 * pot[3:4, :]) * p - 0.5 * beside
         return 0
 
     lax.fori_loop(0, 16, prepare, 0)
-    gram(1 - lax.rem(ids[1], 2), ah, al, ph, lo, er, eh, es, ce, co, out, c, on)
-
-
-def keep_kernel(ids, ph, lo, ah, al, er, eh, es, ce, co, out, c, on):
-    gram(lax.rem(ids[1], 2), ah, al, ph, lo, er, eh, es, ce, co, out, c, on)
+
+    def corr(v, i, j):
+        i, j, x = slice(i, i + 256), slice(j, j + 256), slice(384, 512)
+        acc = dot(ah[i, x], ah[j, x]) + dot(ah[i, x], al[j, x]) + dot(al[i, x], ah[j, x])
+        return v + acc * volume + slots(es, er, i, j)
+
+    for q in range(2):
+        for n, (i, j) in enumerate(((0, 0), (256, 0), (256, 256))):
+            ce[q, n] = corr(fe[q, n], q * 512 + i, q * 512 + j)
+    for i in (0, 256):
+        for j in (0, 256):
+            co[i : i + 256, j : j + 256] = corr(fo[i : i + 256, j : j + 256], 512 + i, j)
+
+
+def send_kernel(ids, part, xh, zh, ah, al, er, eh, ce, co, out, ph, lo, c, on):
+    volume = 1.0 / (512 * 256)
+    lane = lane_of((64, 128))
+
+    def prepare(g, _):
+        to = pl.ds(pl.multiple_of(place(g) * 64, 64), 64)
+        two = zh[g]
+        ext = jnp.concatenate([two, turn(two, -4)], axis=0)
+        for x in range(4):
+            cols = slice(x * 128, (x + 1) * 128)
+            beside = jnp.where(lane % 8 == 7, turn(ext, 7 - x), jnp.zeros((64, 128), F32)) if x < 3 else xh[g]
+            ph[to, cols], lo[to, cols] = split((part[to, cols] - 0.5 * beside) * volume)
+        return 0
+
+    lax.fori_loop(0, 16, prepare, 0)
+    gram(1 - lax.rem(ids[1], 2), ah, al, ph, lo, er, eh, ce, co, out, c, on)
+
+
+def keep_kernel(ids, ph, lo, ah, al, er, eh, ce, co, out, c, on):
+    gram(lax.rem(ids[1], 2), ah, al, ph, lo, er, eh, ce, co, out, c, on)
 
 
 def first_kernel(ids, keep, mate, s1, s2, s3, own):
@@ -518,18 +532,21 @@
         flops=3 * work,
         mib=16,
     )
-    ahead, above, ah, *came = lax.optimization_barrier((ahead, above, ah, *came))
+    ah, *came = lax.optimization_barrier((ah, *came))
     parts = shape(8, 520, 128)
-    send, *rest = call(
-        send_kernel,
-        (ids, part, ahead, above, pot, ah, al, ce, co, *came),
-        [parts, wide, wide, wide, wide, *ext],
-        quads + [pltpu.VMEM((16, 72, 128), F32), pltpu.VMEM((16, 8, 128), F32)],
-        3 * work,
-        22,
-    )
+    ah, al, part, er, eh, _, ce, co = call(
+        fourth_kernel,
+        (ids, pot, part, ah, al, ce, co, *came),
+        [wide, wide, shape(m, 512), *ext, shape(2, 3, 256, 256), shape(512, 512)],
+        [pltpu.VMEM((16, 72, 128), F32), pltpu.VMEM((16, 8, 128), F32)],
+        2 * work,
+        20,
+    )
+    corr = (ah, al, er, eh, ce, co)
+    ahead, above, corr = lax.optimization_barrier((ahead, above, corr))
+    send, ph, lo = call(send_kernel, (ids, part, ahead, above, *corr), [parts, wide, wide], quads, 3 * work, 20)
     mate = lax.ppermute(send, "dom", [(i, i ^ 1) for i in range(16)])
-    keep = call(keep_kernel, (ids, *rest, ce, co), [parts], quads, 3 * work, 18)
+    keep = call(keep_kernel, (ids, ph, lo, *corr), [parts], quads, 3 * work, 18)
     parts = reduced_over_dom(ids, keep, mate)
     parts = lax.all_to_all(parts, "band", 0, 0, tiled=True)
     own = call(finish_kernel, (ids, parts), (shape(64, 128),))

time: 186 us -> 170 us (0.914)
  waiting for transfers between devices: 62.8 us -> 36.2 us
  blocking collectives: 17.7 us -> 21.6 us
  Pallas kernels: 34.6 us -> 37.1 us
    all_to_all x1, waiting for transfers between devices: 36.2 us -> 0.01 us  [on_device(): slab = lax.all_to_all(parts, 'band', 0, 0, tiled=True)]
    ppermute x15, waiting for transfers between devices: 1.25 us -> 13 us  [on_device(): lax.ppermute(came[i], 'band', [(j, band_at(j, move)) for j in range(16)])]
    ppermute x1, starting transfers between devices: 7.1 us -> 0.3 us  [on_device(): mate = lax.ppermute(send, 'dom', [(i, i ^ 1) for i in range(16)])]
    ppermute x15, starting transfers between devices: 27.5 us -> 33.6 us  [on_device(): lax.ppermute(came[i], 'band', [(j, band_at(j, move)) for j in range(16)])]
    all_to_all x1, blocking collectives: 17.7 us -> 21.6 us  [on_device(): parts = lax.all_to_all(parts, 'band', 0, 0, tiled=True)]
    pallas_call x12 -> x13, Pallas kernels: 28.4 us -> 30.9 us  [call(): pl.pallas_call(kernel, out_shape=outs[0] if single else outs, in_specs=sp...]
    ppermute x1, starting transfers between devices: 2.73 us -> 5.05 us  [on_device(): lax.ppermute(first, 'dom', back)]
  transfers between devices with their start and end apart: 31 -> 31, of which waited for: 11 -> 10; matrix products, arithmetic and copies ran while one was open for 0% -> 0% of each run, Pallas kernels for 9% -> 12%
where the time goes in v2:
time: 170 us; the launch traced here: 168 us
  starting transfers between devices  68.8 us (40%)
  Pallas kernels  37.1 us (22%)
  waiting for transfers between devices  36.2 us (21%)
  blocking collectives  21.6 us (13%)
  local copies, waits for them, and re-layouts  3.29 us (2%)
    ppermute x15, starting transfers between devices, on_device(): lax.ppermute(came[i], 'band', [(j, band_at(j, move)) for j in range(16)])  33.6 us
    pallas_call x13, Pallas kernels, call(): pl.pallas_call(kernel, out_shape=outs[0] if single else outs, in_specs=sp...  30.9 us
    all_to_all x1, blocking collectives, on_device(): parts = lax.all_to_all(parts, 'band', 0, 0, tiled=True)  21.6 us
    ppermute x6, waiting for transfers between devices, reduced_over_dom(): got = [lax.ppermute(v, 'dom', moves(*s)) for v, s in zip(sends, steps)]  17.5 us
    ppermute x15, waiting for transfers between devices, on_device(): lax.ppermute(came[i], 'band', [(j, band_at(j, move)) for j in range(16)])  13 us
    ppermute x6, starting transfers between devices, reduced_over_dom(): got = [lax.ppermute(v, 'dom', moves(*s)) for v, s in zip(sends, steps)]  11.5 us
    all_to_all x1, starting transfers between devices, on_device(): slab = lax.all_to_all(parts, 'band', 0, 0, tiled=True)  10.3 us
    pallas_call x1, Pallas kernels, on_device(): pl.pallas_call(spread_kernel, out_shape=[shape(16, 3 * bands, 128), shape...  6.18 us
  transfers between devices with their start and end apart: 31, of which 10 were waited for; matrix products, arithmetic and copies ran while one was open for 0% of the time, Pallas kernels for 12%

profile of v2, /device:TPU:1, one launch (start us, length us, event | category | flops | bytes accessed | tf_op | source)
XLA Modules:
  0.0 168.0 jit_solution(10141175317493127432)
XLA Ops:
  0.6 6.2 %shard_map.77 = (f32[16,192,128]{2,1,0:T(8,128)}, f32[16,64,128]{2,1,0:T(8,128)}) custom-call(f32[4096,128]{1,0:T(8,128)} %bitcast.4), custom_call_target="tpu_custom_call" | custom-call | tf_op jit(solution)/shard_map/pallas_call | solution.py:483
  6.9 10.3 %all-to-all-start = ((f32[16,192,128]{2,1,0:T(8,128)}), f32[16,192,128]{2,1,0:T(8,128)S(1)}, u32[]{:S(2)}, u32[]{:S(2)}) async-start(f32[16,192,128]{2,1,0:T(8,128)} %get-tuple-element.74), calls=%async_computation | async-start | bytes 3145728 | tf_op jit(solution)/shard_map/all_to_all | solution.py:495
  17.4 1.6 copy-done
  19.0 1.7 copy-done.1
  20.7 7.6 %shard_map.79 = (f32[4,128]{1,0:T(4,128)S(1)}, f32[80,128]{1,0:T(8,128)S(1)}, f32[80,128]{1,0:T(8,128)S(1)}, f32[80,128]{1,0:T(8,128)S(1)}, f32[80,128]{1,0:T(8,...) custom-call(s32[2]{0:T(128)S(1)} %pad_add_fusion.ids, ...), custom_call_target="tpu_custom_call" | custom-call | flops 46153920 | bytes 5769240 | tf_op jit(solution)/shard_map/pallas_call | solution.py:439
  28.3 5.4 %collective-permute-start = (f32[80,128]{1,0:T(8,128)S(1)}, f32[80,128]{1,0:T(8,128)S(1)}, u32[]{:S(2)}, u32[]{:S(2)}) collective-permute-start(f32[80,128]{1,0:T(8,128)S(1)} %get-tuple-element.85), channel_id=1, source_target_pairs={{0,64},{16,80},{32,96},{48,112},{64,0},{80,16},{96,32},{112,48},{1... | collective-permute-start | bytes 122888 | tf_op jit(solution)/shard_map/ppermute | solution.py:510
  33.6 1.2 collective-permute-start.1
  34.8 3.0 %collective-permute-start.2 = (f32[80,128]{1,0:T(8,128)S(1)}, f32[80,128]{1,0:T(8,128)S(1)}, u32[]{:S(2)}, u32[]{:S(2)}) collective-permute-start(f32[80,128]{1,0:T(8,128)S(1)} %get-tuple-element.87), channel_id=1, source_target_pairs={{0,48},{16,64},{32,80},{48,96},{64,112},{80,0},{96,16},{112,32},{1... | collective-permute-start | bytes 122888 | tf_op jit(solution)/shard_map/ppermute | solution.py:510
  37.8 2.4 %collective-permute-start.3 = (f32[80,128]{1,0:T(8,128)S(1)}, f32[80,128]{1,0:T(8,128)S(1)}, u32[]{:S(2)}, u32[]{:S(2)}) collective-permute-start(f32[80,128]{1,0:T(8,128)S(1)} %get-tuple-element.88), channel_id=1, source_target_pairs={{0,176},{16,192},{32,208},{48,224},{64,240},{80,128},{96,144},{112... | collective-permute-start | bytes 122888 | tf_op jit(solution)/shard_map/ppermute | solution.py:510
  40.2 2.1 %collective-permute-start.4 = (f32[80,128]{1,0:T(8,128)S(1)}, f32[80,128]{1,0:T(8,128)S(1)}, u32[]{:S(2)}, u32[]{:S(2)}) collective-permute-start(f32[80,128]{1,0:T(8,128)S(1)} %get-tuple-element.89), channel_id=1, source_target_pairs={{0,80},{16,96},{32,112},{48,0},{64,16},{80,32},{96,48},{112,64},{1... | collective-permute-start | bytes 122888 | tf_op jit(solution)/shard_map/ppermute | solution.py:510
  42.3 13.0 %collective-permute-done.refs_1_ = f32[80,128]{1,0:T(8,128)S(1)} collective-permute-done((f32[80,128]{1,0:T(8,128)S(1)}, f32[80,128]{1,0:T(8,128)S(1)}, u32[]{:S(2)}, u32[]{:S(2)}) %collective-permute-start) | collective-permute-done | bytes 40992 | tf_op jit(solution)/shard_map/ppermute | solution.py:510
  55.3 3.8 %collective-permute-start.5 = (f32[80,128]{1,0:T(8,128)S(1)}, f32[80,128]{1,0:T(8,128)S(1)}, u32[]{:S(2)}, u32[]{:S(2)}) collective-permute-start(f32[80,128]{1,0:T(8,128)S(1)} %get-tuple-element.90), channel_id=1, source_target_pairs={{0,208},{16,224},{32,240},{48,128},{64,144},{80,160},{96,176},{112... | collective-permute-start | bytes 122888 | tf_op jit(solution)/shard_map/ppermute | solution.py:510
  59.1 1.5 collective-permute-start.6
  60.6 4.5 %collective-permute-start.7 = (f32[80,128]{1,0:T(8,128)S(1)}, f32[80,128]{1,0:T(8,128)S(1)}, u32[]{:S(2)}, u32[]{:S(2)}) collective-permute-start(f32[80,128]{1,0:T(8,128)S(1)} %get-tuple-element.92), channel_id=1, source_target_pairs={{0,160},{16,176},{32,192},{48,208},{64,224},{80,240},{96,128},{112... | collective-permute-start | bytes 122888 | tf_op jit(solution)/shard_map/ppermute | solution.py:510
  65.2 2.0 %collective-permute-start.9 = (f32[80,128]{1,0:T(8,128)S(1)}, f32[80,128]{1,0:T(8,128)S(1)}, u32[]{:S(2)}, u32[]{:S(2)}) collective-permute-start(f32[80,128]{1,0:T(8,128)S(1)} %get-tuple-element.94), channel_id=1, source_target_pairs={{0,224},{16,240},{32,128},{48,144},{64,160},{80,176},{96,192},{112... | collective-permute-start | bytes 122888 | tf_op jit(solution)/shard_map/ppermute | solution.py:510
  67.1 2.7 %collective-permute-start.10 = (f32[80,128]{1,0:T(8,128)S(1)}, f32[80,128]{1,0:T(8,128)S(1)}, u32[]{:S(2)}, u32[]{:S(2)}) collective-permute-start(f32[80,128]{1,0:T(8,128)S(1)} %get-tuple-element.95), channel_id=1, source_target_pairs={{0,16},{16,32},{32,48},{48,64},{64,80},{80,96},{96,112},{112,0},{1... | collective-permute-start | bytes 122888 | tf_op jit(solution)/shard_map/ppermute | solution.py:510
  70.2 5.0 %collective-permute-start.15 = (f32[16,64,128]{2,1,0:T(8,128)S(1)}, f32[16,64,128]{2,1,0:T(8,128)S(1)}, u32[]{:S(2)}, u32[]{:S(2)}) collective-permute-start(f32[16,64,128]{2,1,0:T(8,128)S(1)} %shard_map.82), channel_id=1, source_target_pairs={{1,0},{2,1},{3,2},{4,3},{5,4},{6,5},{7,6},{8,7},{9,8},{10,9},{11,1... | collective-permute-start | bytes 1572872 | tf_op jit(solution)/shard_map/ppermute | solution.py:522
  75.2 1.4 shard_map.83
  76.7 2.1 %collective-permute-start.12 = (f32[80,128]{1,0:T(8,128)S(1)}, f32[80,128]{1,0:T(8,128)S(1)}, u32[]{:S(2)}, u32[]{:S(2)}) collective-permute-start(f32[80,128]{1,0:T(8,128)S(1)} %get-tuple-element.97), channel_id=1, source_target_pairs={{0,112},{16,0},{32,16},{48,32},{64,48},{80,64},{96,80},{112,96},{1... | collective-permute-start | bytes 122888 | tf_op jit(solution)/shard_map/ppermute | solution.py:510
  78.7 1.7 %collective-permute-start.13 = (f32[80,128]{1,0:T(8,128)S(1)}, f32[80,128]{1,0:T(8,128)S(1)}, u32[]{:S(2)}, u32[]{:S(2)}) collective-permute-start(f32[80,128]{1,0:T(8,128)S(1)} %get-tuple-element.98), channel_id=1, source_target_pairs={{0,240},{16,128},{32,144},{48,160},{64,176},{80,192},{96,208},{112... | collective-permute-start | bytes 122888 | tf_op jit(solution)/shard_map/ppermute | solution.py:510
  80.5 0.9 collective-permute-start.14
  81.8 4.1 %shard_map.80 = (bf16[1024,384]{1,0:T(8,128)(2,1)S(1)}, bf16[1024,384]{1,0:T(8,128)(2,1)S(1)}, f32[1024,384]{1,0:T(8,128)S(1)}, f32[2,3,256,256]{3,2,1,0:T(8,128)S(1)}, f32[512,512]{1,0:T(8,128)S(1)}) custom-call(f32[16,192,128]{2,1,0:T(8,128)S(1)} %all-to-all-done.r, f32[4,128]{1,0:T(4,128)S(1)} %get-tuple-element.81.pot), custom_call_target="tpu_custom_call" | custom-call | flops 3221225472 | bytes 7342080 | tf_op jit(solution)/shard_map/pallas_call | solution.py:439
  85.9 3.9 %shard_map.81 = (bf16[1024,512]{1,0:T(8,128)(2,1)S(1)}, bf16[1024,512]{1,0:T(8,128)(2,1)S(1)}, f32[1024,512]{1,0:T(8,128)S(1)}, bf16[32,1024]{1,0:T(8,128)(2,1)S...) custom-call(s32[2]{0:T(128)S(1)} %pad_add_fusion.ids, ...), custom_call_target="tpu_custom_call" | custom-call | flops 2147483648 | bytes 13436936 | tf_op jit(solution)/shard_map/pallas_call | solution.py:439
  89.9 6.0 %shard_map.84 = (f32[8,520,128]{2,1,0:T(8,128)S(1)}, bf16[1024,512]{1,0:T(8,128)(2,1)S(1)}, bf16[1024,512]{1,0:T(8,128)(2,1)S(1)}) custom-call(s32[2]{0:T(128)S(1)} %pad_add_fusion.ids, f32[1024,512]{1,0:T(8,128)S(1)} %get-tuple-element.120.part, f32[16,64,128]{2,1,0:T(8,128)S(1)} %collective-permute-done.15.xh, ...), custom_call_target="tpu_custom_call" | custom-call | flops 3221225472 | bytes 11960328 | tf_op jit(solution)/shard_map/pallas_call | solution.py:439
  96.2 2.9 %shard_map.85.keep = f32[8,520,128]{2,1,0:T(8,128)S(1)} custom-call(s32[2]{0:T(128)S(1)} %pad_add_fusion.ids, bf16[1024,512]{1,0:T(8,128)(2,1)S(1)} %get-tuple-element.135.ph, bf16[1024,512]{1,0:T(8,128)(2,1)S(1)} %get-tuple-element.136.lo, bf16[1024,512]{1,0:T(8,128)(2,1)S(1)} %get-tuple-element.129.ah, bf16[1024,512]{1,0:T(8,128)(2,1)S(1)} %get-tuple-element.130.al, ...), custom_call_target="tpu_custom_call" | custom-call | flops 3221225472 | bytes 9076744 | tf_op jit(solution)/shard_map/pallas_call | solution.py:439
  99.1 1.1 collective-permute-done.17.mate
  100.2 0.9 shard_map.86
  101.1 2.7 %collective-permute-start.18 = (f32[2,520,128]{2,1,0:T(8,128)S(1)}, f32[2,520,128]{2,1,0:T(8,128)S(1)}, u32[]{:S(2)}, u32[]{:S(2)}) collective-permute-start(f32[2,520,128]{2,1,0:T(8,128)S(1)} %get-tuple-element.139), channel_id=1, source_target_pairs={{0,4},{1,3},{2,6},{3,1},{4,8},{5,7},{6,10},{7,5},{8,12},{9,11},{10... | collective-permute-start | bytes 1597448 | tf_op jit(solution)/shard_map/ppermute | solution.py:468
  104.1 0.7 collective-permute-start.20
  104.8 6.0 %collective-permute-done.18.r1 = f32[2,520,128]{2,1,0:T(8,128)S(1)} collective-permute-done((f32[2,520,128]{2,1,0:T(8,128)S(1)}, f32[2,520,128]{2,1,0:T(8,128)S(1)}, u32[]{:S(2)}, u32[]{:S(2)}) %collective-permute-start.18) | collective-permute-done | bytes 532512 | tf_op jit(solution)/shard_map/ppermute | solution.py:468
  110.8 6.0 %collective-permute-done.19.r2 = f32[2,520,128]{2,1,0:T(8,128)S(1)} collective-permute-done((f32[2,520,128]{2,1,0:T(8,128)S(1)}, f32[2,520,128]{2,1,0:T(8,128)S(1)}, u32[]{:S(2)}, u32[]{:S(2)}) %collective-permute-start.19) | collective-permute-done | bytes 532512 | tf_op jit(solution)/shard_map/ppermute | solution.py:468
  116.8 0.7 shard_map.87
  117.5 1.0 collective-permute-start.21
  118.5 3.7 %collective-permute-start.22 = (f32[520,128]{1,0:T(8,128)S(1)}, f32[520,128]{1,0:T(8,128)S(1)}, u32[]{:S(2)}, u32[]{:S(2)}) collective-permute-start(f32[520,128]{1,0:T(8,128)S(1)} %get-tuple-element.144), channel_id=1, source_target_pairs={{1,13},{3,15},{5,1},{7,3},{9,5},{11,7},{13,9},{15,11},{17,29},{19,... | collective-permute-start | bytes 798728 | tf_op jit(solution)/shard_map/ppermute | solution.py:471
  122.1 3.2 %collective-permute-start.23 = (f32[520,128]{1,0:T(8,128)S(1)}, f32[520,128]{1,0:T(8,128)S(1)}, u32[]{:S(2)}, u32[]{:S(2)}) collective-permute-start(f32[520,128]{1,0:T(8,128)S(1)} %get-tuple-element.145), channel_id=1, source_target_pairs={{1,9},{3,11},{5,13},{7,15},{9,1},{11,3},{13,5},{15,7},{17,25},{19,... | collective-permute-start | bytes 798728 | tf_op jit(solution)/shard_map/ppermute | solution.py:471
  125.9 4.9 %collective-permute-done.23.r3 = f32[520,128]{1,0:T(8,128)S(1)} collective-permute-done((f32[520,128]{1,0:T(8,128)S(1)}, f32[520,128]{1,0:T(8,128)S(1)}, u32[]{:S(2)}, u32[]{:S(2)}) %collective-permute-start.23) | collective-permute-done | bytes 266272 | tf_op jit(solution)/shard_map/ppermute | solution.py:471
  130.8 1.0 shard_map.88
  131.8 21.6 %all_to_all.10.parts = f32[16,64,128]{2,1,0:T(8,128)S(1)} all-to-all(f32[16,64,128]{2,1,0:T(8,128)S(1)} %shard_map.88), channel_id=1, replica_groups=mesh['band'=16,'dom'=16] {'band'}, dimensions={0} | all-to-all | bytes 1048576 | tf_op jit(solution)/shard_map/all_to_all | solution.py:551
  153.4 0.7 shard_map.89.a
  154.1 1.3 collective-permute-start.25
  155.5 2.3 %collective-permute-start.24 = (f32[64,128]{1,0:T(8,128)S(1)}, f32[64,128]{1,0:T(8,128)S(1)}, u32[]{:S(2)}, u32[]{:S(2)}) collective-permute-start(f32[64,128]{1,0:T(8,128)S(1)} %shard_map.89.a), channel_id=1, source_target_pairs={{0,1},{1,0},{2,3},{3,2},{4,5},{5,4},{6,7},{7,6},{8,9},{9,8},{10,11... | collective-permute-start | bytes 98312 | tf_op jit(solution)/shard_map/ppermute | solution.py:553
  157.8 1.2 collective-permute-done.26.d
  159.0 1.5 collective-permute-start.29
  160.4 1.8 %collective-permute-start.28 = (f32[4,64,128]{2,1,0:T(8,128)S(1)}, f32[4,64,128]{2,1,0:T(8,128)S(1)}, u32[]{:S(2)}, u32[]{:S(2)}) collective-permute-start(f32[4,64,128]{2,1,0:T(8,128)S(1)} %shard_map.90.own), channel_id=1, source_target_pairs={{8,0},{9,1},{10,2},{11,3},{12,4},{13,5},{14,6},{15,7},{0,8},{1,9},... | collective-permute-start | bytes 393224 | tf_op jit(solution)/shard_map/ppermute | solution.py:555
  162.2 0.7 collective-permute-start.27
  162.9 1.2 collective-permute-done.29.r3
  164.1 2.0 %collective-permute-done.28.r2 = f32[4,64,128]{2,1,0:T(8,128)S(1)} collective-permute-done((f32[4,64,128]{2,1,0:T(8,128)S(1)}, f32[4,64,128]{2,1,0:T(8,128)S(1)}, u32[]{:S(2)}, u32[]{:S(2)}) %collective-permute-start.28) | collective-permute-done | bytes 131104 | tf_op jit(solution)/shard_map/ppermute | solution.py:555
  166.4 1.6 shard_map.91
  (47 shorter events, 2.6 us)
Async XLA Ops:
  6.8 10.3 %copy-start.5 = (f32[4,18,18]{2,0,1:T(4,128)S(1)}, f32[4,18,18]{2,0,1:T(4,128)}, u32[]{:S(2)}) copy-start(f32[4,18,18]{2,0,1:T(4,128)} %param.9) | copy-start | bytes 15556
  6.8 10.3 %copy-start.6 = (f32[4,18,18]{2,0,1:T(4,128)S(1)}, f32[4,18,18]{2,0,1:T(4,128)}, u32[]{:S(2)}) copy-start(f32[4,18,18]{2,0,1:T(4,128)} %param.10) | copy-start | bytes 15556
  6.8 10.6 %copy-start.2 = (f32[16,64,128]{2,1,0:T(8,128)S(1)}, f32[16,64,128]{2,1,0:T(8,128)}, u32[]{:S(2)}) copy-start(f32[16,64,128]{2,1,0:T(8,128)} %get-tuple-element.80.last) | copy-start | bytes 1572868
  6.9 10.5 %copy-start.3 = (f32[4,16,128]{2,1,0:T(8,128)S(1)}, f32[4,16,128]{2,1,0:T(8,128)}, u32[]{:S(2)}) copy-start(f32[4,16,128]{2,1,0:T(8,128)} %potential) | copy-start | bytes 98308
  6.9 10.5 %copy-start.4 = (s32[4]{0:T(128)S(1)}, s32[4]{0:T(128)}, u32[]{:S(2)}) copy-start(s32[4]{0:T(128)} %count.1) | copy-start | bytes 52
  6.9 63.3 %all-to-all-start = ((f32[16,192,128]{2,1,0:T(8,128)}), f32[16,192,128]{2,1,0:T(8,128)S(1)}, u32[]{:S(2)}, u32[]{:S(2)}) async-start(f32[16,192,128]{2,1,0:T(8,128)} %get-tuple-element.74), calls=%async_computation | async-start | bytes 3145728 | tf_op jit(solution)/shard_map/all_to_all | solution.py:495
  17.4 1.6 copy-start
  19.0 1.7 copy-start.1
  28.3 27.0 %collective-permute-start = (f32[80,128]{1,0:T(8,128)S(1)}, f32[80,128]{1,0:T(8,128)S(1)}, u32[]{:S(2)}, u32[]{:S(2)}) collective-permute-start(f32[80,128]{1,0:T(8,128)S(1)} %get-tuple-element.85), channel_id=1, source_target_pairs={{0,64},{16,80},{32,96},{48,112},{64,0},{80,16},{96,32},{112,48},{1... | collective-permute-start | bytes 122888 | tf_op jit(solution)/shard_map/ppermute | solution.py:510
  33.6 25.5 %collective-permute-start.1 = (f32[80,128]{1,0:T(8,128)S(1)}, f32[80,128]{1,0:T(8,128)S(1)}, u32[]{:S(2)}, u32[]{:S(2)}) collective-permute-start(f32[80,128]{1,0:T(8,128)S(1)} %get-tuple-element.86), channel_id=1, source_target_pairs={{0,192},{16,208},{32,224},{48,240},{64,128},{80,144},{96,160},{112... | collective-permute-start | bytes 122888 | tf_op jit(solution)/shard_map/ppermute | solution.py:510
  34.8 25.8 %collective-permute-start.2 = (f32[80,128]{1,0:T(8,128)S(1)}, f32[80,128]{1,0:T(8,128)S(1)}, u32[]{:S(2)}, u32[]{:S(2)}) collective-permute-start(f32[80,128]{1,0:T(8,128)S(1)} %get-tuple-element.87), channel_id=1, source_target_pairs={{0,48},{16,64},{32,80},{48,96},{64,112},{80,0},{96,16},{112,32},{1... | collective-permute-start | bytes 122888 | tf_op jit(solution)/shard_map/ppermute | solution.py:510
  37.8 27.3 %collective-permute-start.3 = (f32[80,128]{1,0:T(8,128)S(1)}, f32[80,128]{1,0:T(8,128)S(1)}, u32[]{:S(2)}, u32[]{:S(2)}) collective-permute-start(f32[80,128]{1,0:T(8,128)S(1)} %get-tuple-element.88), channel_id=1, source_target_pairs={{0,176},{16,192},{32,208},{48,224},{64,240},{80,128},{96,144},{112... | collective-permute-start | bytes 122888 | tf_op jit(solution)/shard_map/ppermute | solution.py:510
  40.2 25.0 %collective-permute-start.4 = (f32[80,128]{1,0:T(8,128)S(1)}, f32[80,128]{1,0:T(8,128)S(1)}, u32[]{:S(2)}, u32[]{:S(2)}) collective-permute-start(f32[80,128]{1,0:T(8,128)S(1)} %get-tuple-element.89), channel_id=1, source_target_pairs={{0,80},{16,96},{32,112},{48,0},{64,16},{80,32},{96,48},{112,64},{1... | collective-permute-start | bytes 122888 | tf_op jit(solution)/shard_map/ppermute | solution.py:510
  55.3 11.9 %collective-permute-start.5 = (f32[80,128]{1,0:T(8,128)S(1)}, f32[80,128]{1,0:T(8,128)S(1)}, u32[]{:S(2)}, u32[]{:S(2)}) collective-permute-start(f32[80,128]{1,0:T(8,128)S(1)} %get-tuple-element.90), channel_id=1, source_target_pairs={{0,208},{16,224},{32,240},{48,128},{64,144},{80,160},{96,176},{112... | collective-permute-start | bytes 122888 | tf_op jit(solution)/shard_map/ppermute | solution.py:510
  59.1 10.8 %collective-permute-start.6 = (f32[80,128]{1,0:T(8,128)S(1)}, f32[80,128]{1,0:T(8,128)S(1)}, u32[]{:S(2)}, u32[]{:S(2)}) collective-permute-start(f32[80,128]{1,0:T(8,128)S(1)} %get-tuple-element.91), channel_id=1, source_target_pairs={{0,32},{16,48},{32,64},{48,80},{64,96},{80,112},{96,0},{112,16},{1... | collective-permute-start | bytes 122888 | tf_op jit(solution)/shard_map/ppermute | solution.py:510
  60.6 9.6 %collective-permute-start.7 = (f32[80,128]{1,0:T(8,128)S(1)}, f32[80,128]{1,0:T(8,128)S(1)}, u32[]{:S(2)}, u32[]{:S(2)}) collective-permute-start(f32[80,128]{1,0:T(8,128)S(1)} %get-tuple-element.92), channel_id=1, source_target_pairs={{0,160},{16,176},{32,192},{48,208},{64,224},{80,240},{96,128},{112... | collective-permute-start | bytes 122888 | tf_op jit(solution)/shard_map/ppermute | solution.py:510
  65.1 11.5 %collective-permute-start.8 = (f32[80,128]{1,0:T(8,128)S(1)}, f32[80,128]{1,0:T(8,128)S(1)}, u32[]{:S(2)}, u32[]{:S(2)}) collective-permute-start(f32[80,128]{1,0:T(8,128)S(1)} %get-tuple-element.93), channel_id=1, source_target_pairs={{0,96},{16,112},{32,0},{48,16},{64,32},{80,48},{96,64},{112,80},{1... | collective-permute-start | bytes 122888 | tf_op jit(solution)/shard_map/ppermute | solution.py:510
  65.2 13.6 %collective-permute-start.9 = (f32[80,128]{1,0:T(8,128)S(1)}, f32[80,128]{1,0:T(8,128)S(1)}, u32[]{:S(2)}, u32[]{:S(2)}) collective-permute-start(f32[80,128]{1,0:T(8,128)S(1)} %get-tuple-element.94), channel_id=1, source_target_pairs={{0,224},{16,240},{32,128},{48,144},{64,160},{80,176},{96,192},{112... | collective-permute-start | bytes 122888 | tf_op jit(solution)/shard_map/ppermute | solution.py:510
  67.1 13.3 %collective-permute-start.10 = (f32[80,128]{1,0:T(8,128)S(1)}, f32[80,128]{1,0:T(8,128)S(1)}, u32[]{:S(2)}, u32[]{:S(2)}) collective-permute-start(f32[80,128]{1,0:T(8,128)S(1)} %get-tuple-element.95), channel_id=1, source_target_pairs={{0,16},{16,32},{32,48},{48,64},{64,80},{80,96},{96,112},{112,0},{1... | collective-permute-start | bytes 122888 | tf_op jit(solution)/shard_map/ppermute | solution.py:510
  69.9 11.5 %collective-permute-start.11 = (f32[80,128]{1,0:T(8,128)S(1)}, f32[80,128]{1,0:T(8,128)S(1)}, u32[]{:S(2)}, u32[]{:S(2)}) collective-permute-start(f32[80,128]{1,0:T(8,128)S(1)} %get-tuple-element.96), channel_id=1, source_target_pairs={{0,144},{16,160},{32,176},{48,192},{64,208},{80,224},{96,240},{112... | collective-permute-start | bytes 122888 | tf_op jit(solution)/shard_map/ppermute | solution.py:510
  70.2 19.7 %collective-permute-start.15 = (f32[16,64,128]{2,1,0:T(8,128)S(1)}, f32[16,64,128]{2,1,0:T(8,128)S(1)}, u32[]{:S(2)}, u32[]{:S(2)}) collective-permute-start(f32[16,64,128]{2,1,0:T(8,128)S(1)} %shard_map.82), channel_id=1, source_target_pairs={{1,0},{2,1},{3,2},{4,3},{5,4},{6,5},{7,6},{8,7},{9,8},{10,9},{11,1... | collective-permute-start | bytes 1572872 | tf_op jit(solution)/shard_map/ppermute | solution.py:522
  76.7 9.3 %collective-permute-start.12 = (f32[80,128]{1,0:T(8,128)S(1)}, f32[80,128]{1,0:T(8,128)S(1)}, u32[]{:S(2)}, u32[]{:S(2)}) collective-permute-start(f32[80,128]{1,0:T(8,128)S(1)} %get-tuple-element.97), channel_id=1, source_target_pairs={{0,112},{16,0},{32,16},{48,32},{64,48},{80,64},{96,80},{112,96},{1... | collective-permute-start | bytes 122888 | tf_op jit(solution)/shard_map/ppermute | solution.py:510
  78.7 7.2 %collective-permute-start.13 = (f32[80,128]{1,0:T(8,128)S(1)}, f32[80,128]{1,0:T(8,128)S(1)}, u32[]{:S(2)}, u32[]{:S(2)}) collective-permute-start(f32[80,128]{1,0:T(8,128)S(1)} %get-tuple-element.98), channel_id=1, source_target_pairs={{0,240},{16,128},{32,144},{48,160},{64,176},{80,192},{96,208},{112... | collective-permute-start | bytes 122888 | tf_op jit(solution)/shard_map/ppermute | solution.py:510
  80.5 5.4 %collective-permute-start.14 = (f32[80,128]{1,0:T(8,128)S(1)}, f32[80,128]{1,0:T(8,128)S(1)}, u32[]{:S(2)}, u32[]{:S(2)}) collective-permute-start(f32[80,128]{1,0:T(8,128)S(1)} %get-tuple-element.99), channel_id=1, source_target_pairs={{0,128},{16,144},{32,160},{48,176},{64,192},{80,208},{96,224},{112... | collective-permute-start | bytes 122888 | tf_op jit(solution)/shard_map/ppermute | solution.py:510
  81.4 8.5 %collective-permute-start.16 = (f32[16,32,128]{2,1,0:T(8,128)S(1)}, f32[16,32,128]{2,1,0:T(8,128)S(1)}, u32[]{:S(2)}, u32[]{:S(2)}) collective-permute-start(f32[16,32,128]{2,1,0:T(8,128)S(1)} %shard_map.83), channel_id=1, source_target_pairs={{16,0},{32,16},{48,32},{64,48},{80,64},{96,80},{112,96},{128,112},... | collective-permute-start | bytes 786440 | tf_op jit(solution)/shard_map/ppermute | solution.py:522
  95.9 4.3 %collective-permute-start.17 = (f32[8,520,128]{2,1,0:T(8,128)S(1)}, f32[8,520,128]{2,1,0:T(8,128)S(1)}, u32[]{:S(2)}, u32[]{:S(2)}) collective-permute-start(f32[8,520,128]{2,1,0:T(8,128)S(1)} %get-tuple-element.137), channel_id=1, source_target_pairs={{0,1},{1,0},{2,3},{3,2},{4,5},{5,4},{6,7},{7,6},{8,9},{9,8},{10,11... | collective-permute-start | bytes 6389768 | tf_op jit(solution)/shard_map/ppermute | solution.py:548
  101.1 9.7 %collective-permute-start.18 = (f32[2,520,128]{2,1,0:T(8,128)S(1)}, f32[2,520,128]{2,1,0:T(8,128)S(1)}, u32[]{:S(2)}, u32[]{:S(2)}) collective-permute-start(f32[2,520,128]{2,1,0:T(8,128)S(1)} %get-tuple-element.139), channel_id=1, source_target_pairs={{0,4},{1,3},{2,6},{3,1},{4,8},{5,7},{6,10},{7,5},{8,12},{9,11},{10... | collective-permute-start | bytes 1597448 | tf_op jit(solution)/shard_map/ppermute | solution.py:468
  103.8 13.0 %collective-permute-start.19 = (f32[2,520,128]{2,1,0:T(8,128)S(1)}, f32[2,520,128]{2,1,0:T(8,128)S(1)}, u32[]{:S(2)}, u32[]{:S(2)}) collective-permute-start(f32[2,520,128]{2,1,0:T(8,128)S(1)} %get-tuple-element.140), channel_id=1, source_target_pairs={{0,12},{1,3},{2,14},{3,1},{4,0},{5,7},{6,2},{7,5},{8,4},{9,11},{10... | collective-permute-start | bytes 1597448 | tf_op jit(solution)/shard_map/ppermute | solution.py:468
  104.1 12.7 %collective-permute-start.20 = (f32[2,520,128]{2,1,0:T(8,128)S(1)}, f32[2,520,128]{2,1,0:T(8,128)S(1)}, u32[]{:S(2)}, u32[]{:S(2)}) collective-permute-start(f32[2,520,128]{2,1,0:T(8,128)S(1)} %get-tuple-element.141), channel_id=1, source_target_pairs={{0,8},{2,10},{4,12},{6,14},{8,0},{10,2},{12,4},{14,6},{16,24},{18,... | collective-permute-start | bytes 1597448 | tf_op jit(solution)/shard_map/ppermute | solution.py:468
  117.5 7.8 %collective-permute-start.21 = (f32[520,128]{1,0:T(8,128)S(1)}, f32[520,128]{1,0:T(8,128)S(1)}, u32[]{:S(2)}, u32[]{:S(2)}) collective-permute-start(f32[520,128]{1,0:T(8,128)S(1)} %get-tuple-element.143), channel_id=1, source_target_pairs={{0,2},{1,5},{2,0},{3,7},{4,6},{5,9},{6,4},{7,11},{8,10},{9,13},{10... | collective-permute-start | bytes 798728 | tf_op jit(solution)/shard_map/ppermute | solution.py:471
  118.5 7.4 %collective-permute-start.22 = (f32[520,128]{1,0:T(8,128)S(1)}, f32[520,128]{1,0:T(8,128)S(1)}, u32[]{:S(2)}, u32[]{:S(2)}) collective-permute-start(f32[520,128]{1,0:T(8,128)S(1)} %get-tuple-element.144), channel_id=1, source_target_pairs={{1,13},{3,15},{5,1},{7,3},{9,5},{11,7},{13,9},{15,11},{17,29},{19,... | collective-permute-start | bytes 798728 | tf_op jit(solution)/shard_map/ppermute | solution.py:471
  122.1 8.7 %collective-permute-start.23 = (f32[520,128]{1,0:T(8,128)S(1)}, f32[520,128]{1,0:T(8,128)S(1)}, u32[]{:S(2)}, u32[]{:S(2)}) collective-permute-start(f32[520,128]{1,0:T(8,128)S(1)} %get-tuple-element.145), channel_id=1, source_target_pairs={{1,9},{3,11},{5,13},{7,15},{9,1},{11,3},{13,5},{15,7},{17,25},{19,... | collective-permute-start | bytes 798728 | tf_op jit(solution)/shard_map/ppermute | solution.py:471
  154.0 4.9 %collective-permute-start.26 = (f32[64,128]{1,0:T(8,128)S(1)}, f32[64,128]{1,0:T(8,128)S(1)}, u32[]{:S(2)}, u32[]{:S(2)}) collective-permute-start(f32[64,128]{1,0:T(8,128)S(1)} %shard_map.89.a), channel_id=1, source_target_pairs={{0,3},{1,2},{2,1},{3,0},{4,7},{5,6},{6,5},{7,4},{8,11},{9,10},{10,... | collective-permute-start | bytes 98312 | tf_op jit(solution)/shard_map/ppermute | solution.py:553
  154.1 4.8 %collective-permute-start.25 = (f32[64,128]{1,0:T(8,128)S(1)}, f32[64,128]{1,0:T(8,128)S(1)}, u32[]{:S(2)}, u32[]{:S(2)}) collective-permute-start(f32[64,128]{1,0:T(8,128)S(1)} %shard_map.89.a), channel_id=1, source_target_pairs={{0,2},{1,3},{2,0},{3,1},{4,6},{5,7},{6,4},{7,5},{8,10},{9,11},{10,... | collective-permute-start | bytes 98312 | tf_op jit(solution)/shard_map/ppermute | solution.py:553
  155.5 3.5 %collective-permute-start.24 = (f32[64,128]{1,0:T(8,128)S(1)}, f32[64,128]{1,0:T(8,128)S(1)}, u32[]{:S(2)}, u32[]{:S(2)}) collective-permute-start(f32[64,128]{1,0:T(8,128)S(1)} %shard_map.89.a), channel_id=1, source_target_pairs={{0,1},{1,0},{2,3},{3,2},{4,5},{5,4},{6,7},{7,6},{8,9},{9,8},{10,11... | collective-permute-start | bytes 98312 | tf_op jit(solution)/shard_map/ppermute | solution.py:553
  159.0 5.1 %collective-permute-start.29 = (f32[4,64,128]{2,1,0:T(8,128)S(1)}, f32[4,64,128]{2,1,0:T(8,128)S(1)}, u32[]{:S(2)}, u32[]{:S(2)}) collective-permute-start(f32[4,64,128]{2,1,0:T(8,128)S(1)} %shard_map.90.own), channel_id=1, source_target_pairs={{12,0},{13,1},{14,2},{15,3},{0,4},{1,5},{2,6},{3,7},{4,8},{5,9},{6... | collective-permute-start | bytes 393224 | tf_op jit(solution)/shard_map/ppermute | solution.py:555
  160.4 5.7 %collective-permute-start.28 = (f32[4,64,128]{2,1,0:T(8,128)S(1)}, f32[4,64,128]{2,1,0:T(8,128)S(1)}, u32[]{:S(2)}, u32[]{:S(2)}) collective-permute-start(f32[4,64,128]{2,1,0:T(8,128)S(1)} %shard_map.90.own), channel_id=1, source_target_pairs={{8,0},{9,1},{10,2},{11,3},{12,4},{13,5},{14,6},{15,7},{0,8},{1,9},... | collective-permute-start | bytes 393224 | tf_op jit(solution)/shard_map/ppermute | solution.py:555
  162.2 4.2 %collective-permute-start.27 = (f32[4,64,128]{2,1,0:T(8,128)S(1)}, f32[4,64,128]{2,1,0:T(8,128)S(1)}, u32[]{:S(2)}, u32[]{:S(2)}) collective-permute-start(f32[4,64,128]{2,1,0:T(8,128)S(1)} %shard_map.90.own), channel_id=1, source_target_pairs={{4,0},{5,1},{6,2},{7,3},{8,4},{9,5},{10,6},{11,7},{12,8},{13,9},{1... | collective-permute-start | bytes 393224 | tf_op jit(solution)/shard_map/ppermute | solution.py:555
